TPU v7x, 16 devices: a whole 2x2x2 slice. The times are simulated.
16 devices in a mesh: dp: 2 (over z), sp: 8 (over y, x, core).
Axes of the slice: x: 2, y: 2, z: 2, core: 2. Of those that a mesh axis runs over, the one named last changes fastest.
Arguments:
- hidden: bfloat16 [16, 2048, 2048], P('dp', 'sp'), parts along dimension 0
- grad_out: bfloat16 [16, 2048, 2048], P('dp', 'sp'), parts along dimension 0
- w_query: bfloat16 [2048, 16, 128], replicated
- w_key: bfloat16 [2048, 128], replicated
- w_value: bfloat16 [2048, 128], replicated
- w_out: bfloat16 [16, 128, 2048], replicated
Outputs:
- output 1: bfloat16 [16, 2048, 2048], P('dp', 'sp'), parts along dimension 0
- output 2: bfloat16 [16, 2048, 2048], P('dp', 'sp'), parts along dimension 0
- output 3: float32 [4096, 16, 128], P('dp'), parts along dimension 0
- output 4: float32 [4096, 128], P('dp'), parts along dimension 0
- output 5: float32 [4096, 128], P('dp'), parts along dimension 0
- output 6: float32 [32, 128, 2048], P('dp'), parts along dimension 0
There are 2 independent parts. A program takes and returns all parts, laid end to end along the dimension named above; an argument that names none is the same for every part.
All inputs are finite; a program needn't handle non-finite values.
Results may differ from a plain program's by a relative error of at most 0.02.
Values are sent between devices in bfloat16 or wider.
A program may use at most 1 GiB of HBM per device.

v0:
```python
import jax
import jax.numpy as jnp
from jax import lax
from jax.sharding import PartitionSpec as P

ROPE_BASE = 10000.0
NEG_BIG = -1e30


def rope_tables(positions, head_dim):
    half_dim = head_dim // 2
    inv_freq = ROPE_BASE ** (-jnp.arange(half_dim, dtype=jnp.float32) * (2.0 / head_dim))
    angles = positions.astype(jnp.float32)[:, None] * inv_freq[None, :]
    return jnp.cos(angles), jnp.sin(angles)


def rotate(x_in, cos_t, sin_t):
    half_dim = x_in.shape[-1] // 2
    lead_half = x_in[..., :half_dim]
    tail_half = x_in[..., half_dim:]
    return jnp.concatenate([lead_half * cos_t - tail_half * sin_t, tail_half * cos_t + lead_half * sin_t], axis=-1)


def attend_forward(q_heads, k_all, v_all):
    n_batch, seq_len, heads_loc = q_heads.shape[:3]
    q_rows = min(seq_len, 512)
    col_ids = jnp.arange(seq_len)

    def fwd_block(blk_index, loop_state):
        o_heads, log_norm = loop_state
        row_start = blk_index * q_rows
        q_blk = lax.dynamic_slice_in_dim(q_heads, row_start, q_rows, axis=1)
        scores = jnp.einsum('bqhe,bke->bhqk', q_blk, k_all, preferred_element_type=jnp.float32)
        row_ids = row_start + jnp.arange(q_rows)
        scores = jnp.where(col_ids[None, :] <= row_ids[:, None], scores, NEG_BIG)
        row_max = jnp.max(scores, axis=-1, keepdims=True)
        exp_scores = jnp.exp(scores - row_max)
        row_sum = jnp.sum(exp_scores, axis=-1, keepdims=True)
        attn_probs = (exp_scores / row_sum).astype(jnp.bfloat16)
        o_blk = jnp.einsum('bhqk,bke->bqhe', attn_probs, v_all, preferred_element_type=jnp.float32).astype(jnp.bfloat16)
        norm_blk = (row_max + jnp.log(row_sum))[..., 0]
        o_heads = lax.dynamic_update_slice_in_dim(o_heads, o_blk, row_start, axis=1)
        log_norm = lax.dynamic_update_slice_in_dim(log_norm, norm_blk, row_start, axis=2)
        return o_heads, log_norm

    start_state = (jnp.zeros(q_heads.shape, jnp.bfloat16), jnp.zeros((n_batch, heads_loc, seq_len), jnp.float32))
    return lax.fori_loop(0, seq_len // q_rows, fwd_block, start_state)


def attend_backward(q_heads, k_all, v_all, o_heads, do_heads, log_norm):
    seq_len = q_heads.shape[1]
    q_rows = min(seq_len, 512)
    col_ids = jnp.arange(seq_len)

    def bwd_block(blk_index, loop_state):
        dq_heads, dk_acc, dv_acc = loop_state
        row_start = blk_index * q_rows
        q_blk = lax.dynamic_slice_in_dim(q_heads, row_start, q_rows, axis=1)
        o_blk = lax.dynamic_slice_in_dim(o_heads, row_start, q_rows, axis=1)
        do_blk = lax.dynamic_slice_in_dim(do_heads, row_start, q_rows, axis=1)
        norm_blk = lax.dynamic_slice_in_dim(log_norm, row_start, q_rows, axis=2)
        scores = jnp.einsum('bqhe,bke->bhqk', q_blk, k_all, preferred_element_type=jnp.float32)
        row_ids = row_start + jnp.arange(q_rows)
        scores = jnp.where(col_ids[None, :] <= row_ids[:, None], scores, NEG_BIG)
        attn_probs = jnp.exp(scores - norm_blk[..., None])
        dv_acc = dv_acc + jnp.einsum('bhqk,bqhe->bke', attn_probs.astype(jnp.bfloat16), do_blk, preferred_element_type=jnp.float32)
        d_probs = jnp.einsum('bqhe,bke->bhqk', do_blk, v_all, preferred_element_type=jnp.float32)
        row_dot = jnp.einsum('bqhe,bqhe->bhq', do_blk, o_blk, preferred_element_type=jnp.float32)
        d_scores = (attn_probs * (d_probs - row_dot[..., None])).astype(jnp.bfloat16)
        dq_blk = jnp.einsum('bhqk,bke->bqhe', d_scores, k_all, preferred_element_type=jnp.float32).astype(jnp.bfloat16)
        dk_acc = dk_acc + jnp.einsum('bhqk,bqhe->bke', d_scores, q_blk, preferred_element_type=jnp.float32)
        dq_heads = lax.dynamic_update_slice_in_dim(dq_heads, dq_blk, row_start, axis=1)
        return dq_heads, dk_acc, dv_acc

    start_state = (jnp.zeros(q_heads.shape, jnp.bfloat16), jnp.zeros(k_all.shape, jnp.float32), jnp.zeros(k_all.shape, jnp.float32))
    return lax.fori_loop(0, seq_len // q_rows, bwd_block, start_state)


def solution(mesh):
    def local_step(hid_loc, gout_loc, w_query, w_key, w_value, w_out):
        seq_loc = hid_loc.shape[1]
        head_dim = w_query.shape[2]
        q_scale = head_dim ** -0.5
        pos_loc = lax.axis_index('sp') * seq_loc + jnp.arange(seq_loc)
        cos_l, sin_l = rope_tables(pos_loc, head_dim)
        queries = jnp.einsum('bsd,dhe->bshe', hid_loc, w_query, preferred_element_type=jnp.float32).astype(jnp.bfloat16)
        key_proj = jnp.einsum('bsd,de->bse', hid_loc, w_key, preferred_element_type=jnp.float32).astype(jnp.bfloat16)
        val_proj = jnp.einsum('bsd,de->bse', hid_loc, w_value, preferred_element_type=jnp.float32).astype(jnp.bfloat16)
        q_rot = rotate(queries.astype(jnp.float32) * q_scale, cos_l[:, None, :], sin_l[:, None, :]).astype(jnp.bfloat16)
        k_rot = rotate(key_proj.astype(jnp.float32), cos_l, sin_l).astype(jnp.bfloat16)
        q_heads = lax.all_to_all(q_rot, 'sp', 2, 1, tiled=True)
        k_all = lax.all_gather(k_rot, 'sp', axis=1, tiled=True)
        v_all = lax.all_gather(val_proj, 'sp', axis=1, tiled=True)
        o_heads, log_norm = attend_forward(q_heads, k_all, v_all)
        o_pos = lax.all_to_all(o_heads, 'sp', 1, 2, tiled=True)
        attn_out = jnp.einsum('bshe,hed->bsd', o_pos, w_out, preferred_element_type=jnp.float32).astype(jnp.bfloat16)
        dw_out = lax.psum(jnp.einsum('bshe,bsd->hed', o_pos, gout_loc, preferred_element_type=jnp.float32), 'sp')
        do_pos = jnp.einsum('bsd,hed->bshe', gout_loc, w_out, preferred_element_type=jnp.float32).astype(jnp.bfloat16)
        do_heads = lax.all_to_all(do_pos, 'sp', 2, 1, tiled=True)
        dq_heads, dk_acc, dv_acc = attend_backward(q_heads, k_all, v_all, o_heads, do_heads, log_norm)
        dq_pos = lax.all_to_all(dq_heads, 'sp', 1, 2, tiled=True)
        dk_loc = lax.psum_scatter(dk_acc, 'sp', scatter_dimension=1, tiled=True)
        dv_loc = lax.psum_scatter(dv_acc, 'sp', scatter_dimension=1, tiled=True)
        dq_raw = (rotate(dq_pos.astype(jnp.float32), cos_l[:, None, :], -sin_l[:, None, :]) * q_scale).astype(jnp.bfloat16)
        dk_raw = rotate(dk_loc, cos_l, -sin_l).astype(jnp.bfloat16)
        dv_raw = dv_loc.astype(jnp.bfloat16)
        d_hidden = (jnp.einsum('bshe,dhe->bsd', dq_raw, w_query, preferred_element_type=jnp.float32) + jnp.einsum('bse,de->bsd', dk_raw, w_key, preferred_element_type=jnp.float32) + jnp.einsum('bse,de->bsd', dv_raw, w_value, preferred_element_type=jnp.float32)).astype(jnp.bfloat16)
        dw_query = lax.psum(jnp.einsum('bsd,bshe->dhe', hid_loc, dq_raw, preferred_element_type=jnp.float32), 'sp')
        dw_key = lax.psum(jnp.einsum('bsd,bse->de', hid_loc, dk_raw, preferred_element_type=jnp.float32), 'sp')
        dw_value = lax.psum(jnp.einsum('bsd,bse->de', hid_loc, dv_raw, preferred_element_type=jnp.float32), 'sp')
        return attn_out, d_hidden, dw_query, dw_key, dw_value, dw_out

    act_spec = P('dp', 'sp', None)
    return jax.shard_map(local_step, mesh=mesh, in_specs=(act_spec, act_spec, P(), P(), P(), P()), out_specs=(act_spec, act_spec, P('dp', None, None), P('dp', None), P('dp', None), P('dp', None, None)), check_vma=False)
```

profile of v0, /device:TPU:0, one launch (start us, length us, event | category | flops | bytes accessed | tf_op | source)
XLA Modules:
  0.0 1917.8 jit_solution(11215187769855461547)
XLA Ops:
  27.9 21.7 %convert_multiply_fusion = f32[8,256,16,128]{1,3,2,0:T(8,128)S(1)} fusion(bf16[2048,16,128]{0,2,1:T(8,128)(2,1)} %copy.35, bf16[8,256,2048]{2,1,0:T(8,128)(2,1)} %param.10), kind=kOutput, calls=%fused_computation.59 | convolution fusion | flops 17192452096 | bytes 33554432 | tf_op jit(solution)/shard_map/bsd,dhe->bshe/dot_general | solution.py:86
  83.1 23.0 %fusion.66 = bf16[8,256,16,128]{3,1,2,0:T(8,128)(2,1)} fusion(bf16[16,128,2048]{2,1,0:T(8,128)(2,1)} %param.15, bf16[8,256,2048]{2,1,0:T(8,128)(2,1)} %param.11), kind=kOutput, calls=%fused_computation.80 | convolution fusion | flops 17184063488 | bytes 25165824 | tf_op jit(solution)/shard_map/bsd,hed->bshe/dot_general | solution.py:98
  113.9 73.4 %all-to-all-done = bf16[8,256,16,128]{1,3,0,2:T(8,128)(2,1)} async-done(((bf16[8,256,16,128]{1,3,0,2:T(8,128)(2,1)}), bf16[8,256,16,128]{1,3,0,2:T(8,128)(2,1)}, u32[]{:S(2)}, u32[]{:S(2)}) %all-to-all-start) | async-done | bytes 8388640 | tf_op jit(solution)/shard_map/all_to_all | solution.py:91
  215.4 303.1 %while.34 = (s32[]{:T(128)}, bf16[8,2048,2,128]{3,1,2,0:T(8,128)(2,1)}, f32[8,2,2048]{2,1,0:T(2,128)S(1)}, bf16[8,2048,2,128]{3,1,2,0:T(8,128)(2,1)}, bf16[8,204...) while((s32[]{:T(128)}, ...), condition=%wide.region_3.4_spmd.clone, body=%wide.region_0.3_spmd.clone.sunk | while | flops 8743018496 | bytes 218370208 | solution.py:47
  216.1 25.7 %bitcast_reduce_fusion.2 = (f32[8,2,512]{2,1,0:T(2,128)S(1)}, f32[8,512,2,2048]{3,1,2,0:T(8,128)}) fusion(pred[512,2048]{1,0:T(8,128)(4,1)S(1)} %iota_compare_fusion.4, bf16[8,2048,128]{2,1,0:T(8,128)(2,1)} %get-tuple-element.596, bf16[8,2048,2,128]{3,1,2,0:T(8,128)(2,1)} %get-tuple-element.595, s32[]{:T(128)S(6)} %select_n.75), kind=kOutput, calls=%fused_computation.3.clone.1 | convolution fusion | flops 4328513536 | bytes 74481664 | tf_op jit(solution)/shard_map/while/body/eval_jaxpr/bqhe,bke->bhqk/dot_general | solution.py:33
  241.8 21.5 %fusion.123 = f32[8,2,512]{2,1,0:T(2,128)S(1)} fusion(f32[8,512,2,2048]{3,1,2,0:T(8,128)} %get-tuple-element.558, f32[8,2,512]{2,1,0:T(2,128)S(1)} %get-tuple-element.559, pred[512,2048]{1,0:T(8,128)(4,1)S(1)} %iota_compare_fusion.4), kind=kLoop, calls=%fused_computation.6.clone.1 | loop fusion | flops 50323456 | bytes 68222976 | tf_op jit(solution)/shard_map/while/body/eval_jaxpr/reduce_sum | solution.py:38
  263.3 27.8 %bitcast_dynamic-update-slice_fusion.2 = bf16[8,2048,2,128]{3,1,2,0:T(8,128)(2,1)} fusion(bf16[8,2048,2,128]{3,1,2,0:T(8,128)(2,1)} %get-tuple-element.583, s32[]{:T(128)S(6)} %select_n.75, bf16[8,2048,128]{2,1,0:T(8,128)(2,1)} %get-tuple-element.597, f32[8,512,2,2048]{3,1,2,0:T(8,128)} %get-tuple-element.558, f32[8,2,512]{2,1,0:T(2,128)S(1)} %fusion.123, ...), kind=kOutput, calls=%fused_computation.12.clone.1 | convolution fusion | flops 4363124736 | bytes 74514432 | tf_op jit(solution)/shard_map/while/body/eval_jaxpr/bhqk,bke->bqhe/dot_general | solution.py:40
  291.8 25.7 %bitcast_reduce_fusion.2 = (f32[8,2,512]{2,1,0:T(2,128)S(1)}, f32[8,512,2,2048]{3,1,2,0:T(8,128)}) fusion(pred[512,2048]{1,0:T(8,128)(4,1)S(1)} %iota_compare_fusion.4, bf16[8,2048,128]{2,1,0:T(8,128)(2,1)} %get-tuple-element.596, bf16[8,2048,2,128]{3,1,2,0:T(8,128)(2,1)} %get-tuple-element.595, s32[]{:T(128)S(6)} %select_n.75), kind=kOutput, calls=%fused_computation.3.clone.1 | convolution fusion | flops 4328513536 | bytes 74481664 | tf_op jit(solution)/shard_map/while/body/eval_jaxpr/bqhe,bke->bhqk/dot_general | solution.py:33
  317.6 21.5 %fusion.123 = f32[8,2,512]{2,1,0:T(2,128)S(1)} fusion(f32[8,512,2,2048]{3,1,2,0:T(8,128)} %get-tuple-element.558, f32[8,2,512]{2,1,0:T(2,128)S(1)} %get-tuple-element.559, pred[512,2048]{1,0:T(8,128)(4,1)S(1)} %iota_compare_fusion.4), kind=kLoop, calls=%fused_computation.6.clone.1 | loop fusion | flops 50323456 | bytes 68222976 | tf_op jit(solution)/shard_map/while/body/eval_jaxpr/reduce_sum | solution.py:38
  339.1 27.8 %bitcast_dynamic-update-slice_fusion.2 = bf16[8,2048,2,128]{3,1,2,0:T(8,128)(2,1)} fusion(bf16[8,2048,2,128]{3,1,2,0:T(8,128)(2,1)} %get-tuple-element.583, s32[]{:T(128)S(6)} %select_n.75, bf16[8,2048,128]{2,1,0:T(8,128)(2,1)} %get-tuple-element.597, f32[8,512,2,2048]{3,1,2,0:T(8,128)} %get-tuple-element.558, f32[8,2,512]{2,1,0:T(2,128)S(1)} %fusion.123, ...), kind=kOutput, calls=%fused_computation.12.clone.1 | convolution fusion | flops 4363124736 | bytes 74514432 | tf_op jit(solution)/shard_map/while/body/eval_jaxpr/bhqk,bke->bqhe/dot_general | solution.py:40
  367.6 25.7 %bitcast_reduce_fusion.2 = (f32[8,2,512]{2,1,0:T(2,128)S(1)}, f32[8,512,2,2048]{3,1,2,0:T(8,128)}) fusion(pred[512,2048]{1,0:T(8,128)(4,1)S(1)} %iota_compare_fusion.4, bf16[8,2048,128]{2,1,0:T(8,128)(2,1)} %get-tuple-element.596, bf16[8,2048,2,128]{3,1,2,0:T(8,128)(2,1)} %get-tuple-element.595, s32[]{:T(128)S(6)} %select_n.75), kind=kOutput, calls=%fused_computation.3.clone.1 | convolution fusion | flops 4328513536 | bytes 74481664 | tf_op jit(solution)/shard_map/while/body/eval_jaxpr/bqhe,bke->bhqk/dot_general | solution.py:33
  393.3 21.5 %fusion.123 = f32[8,2,512]{2,1,0:T(2,128)S(1)} fusion(f32[8,512,2,2048]{3,1,2,0:T(8,128)} %get-tuple-element.558, f32[8,2,512]{2,1,0:T(2,128)S(1)} %get-tuple-element.559, pred[512,2048]{1,0:T(8,128)(4,1)S(1)} %iota_compare_fusion.4), kind=kLoop, calls=%fused_computation.6.clone.1 | loop fusion | flops 50323456 | bytes 68222976 | tf_op jit(solution)/shard_map/while/body/eval_jaxpr/reduce_sum | solution.py:38
  414.9 27.8 %bitcast_dynamic-update-slice_fusion.2 = bf16[8,2048,2,128]{3,1,2,0:T(8,128)(2,1)} fusion(bf16[8,2048,2,128]{3,1,2,0:T(8,128)(2,1)} %get-tuple-element.583, s32[]{:T(128)S(6)} %select_n.75, bf16[8,2048,128]{2,1,0:T(8,128)(2,1)} %get-tuple-element.597, f32[8,512,2,2048]{3,1,2,0:T(8,128)} %get-tuple-element.558, f32[8,2,512]{2,1,0:T(2,128)S(1)} %fusion.123, ...), kind=kOutput, calls=%fused_computation.12.clone.1 | convolution fusion | flops 4363124736 | bytes 74514432 | tf_op jit(solution)/shard_map/while/body/eval_jaxpr/bhqk,bke->bqhe/dot_general | solution.py:40
  443.4 25.7 %bitcast_reduce_fusion.2 = (f32[8,2,512]{2,1,0:T(2,128)S(1)}, f32[8,512,2,2048]{3,1,2,0:T(8,128)}) fusion(pred[512,2048]{1,0:T(8,128)(4,1)S(1)} %iota_compare_fusion.4, bf16[8,2048,128]{2,1,0:T(8,128)(2,1)} %get-tuple-element.596, bf16[8,2048,2,128]{3,1,2,0:T(8,128)(2,1)} %get-tuple-element.595, s32[]{:T(128)S(6)} %select_n.75), kind=kOutput, calls=%fused_computation.3.clone.1 | convolution fusion | flops 4328513536 | bytes 74481664 | tf_op jit(solution)/shard_map/while/body/eval_jaxpr/bqhe,bke->bhqk/dot_general | solution.py:33
  469.1 21.5 %fusion.123 = f32[8,2,512]{2,1,0:T(2,128)S(1)} fusion(f32[8,512,2,2048]{3,1,2,0:T(8,128)} %get-tuple-element.558, f32[8,2,512]{2,1,0:T(2,128)S(1)} %get-tuple-element.559, pred[512,2048]{1,0:T(8,128)(4,1)S(1)} %iota_compare_fusion.4), kind=kLoop, calls=%fused_computation.6.clone.1 | loop fusion | flops 50323456 | bytes 68222976 | tf_op jit(solution)/shard_map/while/body/eval_jaxpr/reduce_sum | solution.py:38
  490.6 27.8 %bitcast_dynamic-update-slice_fusion.2 = bf16[8,2048,2,128]{3,1,2,0:T(8,128)(2,1)} fusion(bf16[8,2048,2,128]{3,1,2,0:T(8,128)(2,1)} %get-tuple-element.583, s32[]{:T(128)S(6)} %select_n.75, bf16[8,2048,128]{2,1,0:T(8,128)(2,1)} %get-tuple-element.597, f32[8,512,2,2048]{3,1,2,0:T(8,128)} %get-tuple-element.558, f32[8,2,512]{2,1,0:T(2,128)S(1)} %fusion.123, ...), kind=kOutput, calls=%fused_computation.12.clone.1 | convolution fusion | flops 4363124736 | bytes 74514432 | tf_op jit(solution)/shard_map/while/body/eval_jaxpr/bhqk,bke->bqhe/dot_general | solution.py:40
  531.6 579.3 %while.35 = (s32[]{:T(128)}, bf16[8,2048,2,128]{3,2,0,1:T(2,128)(2,1)}, f32[8,2048,128]{2,1,0:T(8,128)}, f32[8,2048,128]{2,1,0:T(8,128)}, bf16[8,2048,2,128]{3,1...) while((s32[]{:T(128)}, ...), condition=%wide.region_5.6_spmd.clone, body=%wide.region_4.5_spmd.clone.sunk | while | flops 21623726080 | bytes 382996672 | solution.py:76
  540.2 26.7 %fusion.134 = f32[8,512,2,2048]{3,1,2,0:T(8,128)} fusion(bf16[8,2048,128]{2,1,0:T(8,128)(2,1)} %get-tuple-element.635, bf16[8,2048,2,128]{3,1,2,0:T(8,128)(2,1)} %get-tuple-element.634, s32[]{:T(128)S(6)} %select_n.78), kind=kOutput, calls=%fused_computation.33.clone.1 | convolution fusion | flops 4294967296 | bytes 73400320 | tf_op jit(solution)/shard_map/while/body/eval_jaxpr/bqhe,bke->bhqk/dot_general | solution.py:62
  567.6 39.2 %fusion.135 = bf16[8,2,512,2048]{3,2,1,0:T(8,128)(2,1)} fusion(f32[8,512,2,2048]{3,1,2,0:T(8,128)} %fusion.134, f32[8,2,512]{2,1,0:T(2,128)S(1)} %copy.107, f32[8,2,512]{2,1,0:T(2,128)S(1)} %constant_dynamic-slice_fusion.3, pred[512,2048]{1,0:T(8,128)(4,1)S(1)} %iota_compare_fusion.5, bf16[8,2048,128]{2,1,0:T(8,128)(2,1)} %get-tuple-element.638, ...), kind=kOutput, calls=%fused_computation.20.clone.2 | convolution fusion | flops 4378853376 | bytes 108068864 | tf_op jit(solution)/shard_map/while/body/eval_jaxpr/bqhe,bke->bhqk/dot_general | solution.py:67
  606.8 16.2 convert_bitcast_fusion.2
  626.5 17.9 bitcast_add_fusion.5
  644.4 29.5 %bitcast_add_fusion.6 = f32[8,2048,128]{2,1,0:T(8,128)} fusion(f32[8,2048,128]{2,1,0:T(8,128)} %get-tuple-element.619, f32[8,512,2,2048]{3,1,2,0:T(8,128)} %fusion.134, f32[8,2,512]{2,1,0:T(2,128)S(1)} %constant_dynamic-slice_fusion.3, pred[512,2048]{1,0:T(8,128)(4,1)S(1)} %iota_compare_fusion.5, pred[]{:T(512)S(6)} %compare.3, ...), kind=kOutput, calls=%fused_computation.28.clone.1 | convolution fusion | flops 4349493248 | bytes 87064584 | tf_op jit(solution)/shard_map/while/body/eval_jaxpr/bhqk,bqhe->bke/dot_general | solution.py:66
  682.1 26.7 %fusion.134 = f32[8,512,2,2048]{3,1,2,0:T(8,128)} fusion(bf16[8,2048,128]{2,1,0:T(8,128)(2,1)} %get-tuple-element.635, bf16[8,2048,2,128]{3,1,2,0:T(8,128)(2,1)} %get-tuple-element.634, s32[]{:T(128)S(6)} %select_n.78), kind=kOutput, calls=%fused_computation.33.clone.1 | convolution fusion | flops 4294967296 | bytes 73400320 | tf_op jit(solution)/shard_map/while/body/eval_jaxpr/bqhe,bke->bhqk/dot_general | solution.py:62
  709.5 39.2 %fusion.135 = bf16[8,2,512,2048]{3,2,1,0:T(8,128)(2,1)} fusion(f32[8,512,2,2048]{3,1,2,0:T(8,128)} %fusion.134, f32[8,2,512]{2,1,0:T(2,128)S(1)} %copy.107, f32[8,2,512]{2,1,0:T(2,128)S(1)} %constant_dynamic-slice_fusion.3, pred[512,2048]{1,0:T(8,128)(4,1)S(1)} %iota_compare_fusion.5, bf16[8,2048,128]{2,1,0:T(8,128)(2,1)} %get-tuple-element.638, ...), kind=kOutput, calls=%fused_computation.20.clone.2 | convolution fusion | flops 4378853376 | bytes 108068864 | tf_op jit(solution)/shard_map/while/body/eval_jaxpr/bqhe,bke->bhqk/dot_general | solution.py:67
  748.7 16.2 convert_bitcast_fusion.2
  768.5 19.7 %bitcast_add_fusion.5 = f32[8,2048,128]{2,1,0:T(8,128)} fusion(f32[8,2048,128]{2,1,0:T(8,128)} %get-tuple-element.618, bf16[8,2,512,2048]{3,2,1,0:T(8,128)(2,1)} %fusion.135, pred[]{:T(512)S(6)} %compare.3, bf16[8,2048,2,128]{3,1,2,0:T(8,128)(2,1)} %get-tuple-element.634, s32[]{:T(128)S(6)} %select_n.78), kind=kOutput, calls=%fused_computation.29.clone.1 | convolution fusion | flops 4299161600 | bytes 52428804 | tf_op jit(solution)/shard_map/while/body/eval_jaxpr/bhqk,bqhe->bke/dot_general | solution.py:71
  788.2 31.3 %bitcast_add_fusion.6 = f32[8,2048,128]{2,1,0:T(8,128)} fusion(f32[8,2048,128]{2,1,0:T(8,128)} %get-tuple-element.619, f32[8,512,2,2048]{3,1,2,0:T(8,128)} %fusion.134, f32[8,2,512]{2,1,0:T(2,128)S(1)} %constant_dynamic-slice_fusion.3, pred[512,2048]{1,0:T(8,128)(4,1)S(1)} %iota_compare_fusion.5, pred[]{:T(512)S(6)} %compare.3, ...), kind=kOutput, calls=%fused_computation.28.clone.1 | convolution fusion | flops 4349493248 | bytes 87064584 | tf_op jit(solution)/shard_map/while/body/eval_jaxpr/bhqk,bqhe->bke/dot_general | solution.py:66
  827.7 26.7 %fusion.134 = f32[8,512,2,2048]{3,1,2,0:T(8,128)} fusion(bf16[8,2048,128]{2,1,0:T(8,128)(2,1)} %get-tuple-element.635, bf16[8,2048,2,128]{3,1,2,0:T(8,128)(2,1)} %get-tuple-element.634, s32[]{:T(128)S(6)} %select_n.78), kind=kOutput, calls=%fused_computation.33.clone.1 | convolution fusion | flops 4294967296 | bytes 73400320 | tf_op jit(solution)/shard_map/while/body/eval_jaxpr/bqhe,bke->bhqk/dot_general | solution.py:62
  855.1 39.2 %fusion.135 = bf16[8,2,512,2048]{3,2,1,0:T(8,128)(2,1)} fusion(f32[8,512,2,2048]{3,1,2,0:T(8,128)} %fusion.134, f32[8,2,512]{2,1,0:T(2,128)S(1)} %copy.107, f32[8,2,512]{2,1,0:T(2,128)S(1)} %constant_dynamic-slice_fusion.3, pred[512,2048]{1,0:T(8,128)(4,1)S(1)} %iota_compare_fusion.5, bf16[8,2048,128]{2,1,0:T(8,128)(2,1)} %get-tuple-element.638, ...), kind=kOutput, calls=%fused_computation.20.clone.2 | convolution fusion | flops 4378853376 | bytes 108068864 | tf_op jit(solution)/shard_map/while/body/eval_jaxpr/bqhe,bke->bhqk/dot_general | solution.py:67
  894.3 16.2 convert_bitcast_fusion.2
  914.1 19.7 %bitcast_add_fusion.5 = f32[8,2048,128]{2,1,0:T(8,128)} fusion(f32[8,2048,128]{2,1,0:T(8,128)} %get-tuple-element.618, bf16[8,2,512,2048]{3,2,1,0:T(8,128)(2,1)} %fusion.135, pred[]{:T(512)S(6)} %compare.3, bf16[8,2048,2,128]{3,1,2,0:T(8,128)(2,1)} %get-tuple-element.634, s32[]{:T(128)S(6)} %select_n.78), kind=kOutput, calls=%fused_computation.29.clone.1 | convolution fusion | flops 4299161600 | bytes 52428804 | tf_op jit(solution)/shard_map/while/body/eval_jaxpr/bhqk,bqhe->bke/dot_general | solution.py:71
  933.8 31.3 %bitcast_add_fusion.6 = f32[8,2048,128]{2,1,0:T(8,128)} fusion(f32[8,2048,128]{2,1,0:T(8,128)} %get-tuple-element.619, f32[8,512,2,2048]{3,1,2,0:T(8,128)} %fusion.134, f32[8,2,512]{2,1,0:T(2,128)S(1)} %constant_dynamic-slice_fusion.3, pred[512,2048]{1,0:T(8,128)(4,1)S(1)} %iota_compare_fusion.5, pred[]{:T(512)S(6)} %compare.3, ...), kind=kOutput, calls=%fused_computation.28.clone.1 | convolution fusion | flops 4349493248 | bytes 87064584 | tf_op jit(solution)/shard_map/while/body/eval_jaxpr/bhqk,bqhe->bke/dot_general | solution.py:66
  973.3 26.7 %fusion.134 = f32[8,512,2,2048]{3,1,2,0:T(8,128)} fusion(bf16[8,2048,128]{2,1,0:T(8,128)(2,1)} %get-tuple-element.635, bf16[8,2048,2,128]{3,1,2,0:T(8,128)(2,1)} %get-tuple-element.634, s32[]{:T(128)S(6)} %select_n.78), kind=kOutput, calls=%fused_computation.33.clone.1 | convolution fusion | flops 4294967296 | bytes 73400320 | tf_op jit(solution)/shard_map/while/body/eval_jaxpr/bqhe,bke->bhqk/dot_general | solution.py:62
  1000.7 39.2 %fusion.135 = bf16[8,2,512,2048]{3,2,1,0:T(8,128)(2,1)} fusion(f32[8,512,2,2048]{3,1,2,0:T(8,128)} %fusion.134, f32[8,2,512]{2,1,0:T(2,128)S(1)} %copy.107, f32[8,2,512]{2,1,0:T(2,128)S(1)} %constant_dynamic-slice_fusion.3, pred[512,2048]{1,0:T(8,128)(4,1)S(1)} %iota_compare_fusion.5, bf16[8,2048,128]{2,1,0:T(8,128)(2,1)} %get-tuple-element.638, ...), kind=kOutput, calls=%fused_computation.20.clone.2 | convolution fusion | flops 4378853376 | bytes 108068864 | tf_op jit(solution)/shard_map/while/body/eval_jaxpr/bqhe,bke->bhqk/dot_general | solution.py:67
  1039.9 16.2 convert_bitcast_fusion.2
  1059.6 19.7 %bitcast_add_fusion.5 = f32[8,2048,128]{2,1,0:T(8,128)} fusion(f32[8,2048,128]{2,1,0:T(8,128)} %get-tuple-element.618, bf16[8,2,512,2048]{3,2,1,0:T(8,128)(2,1)} %fusion.135, pred[]{:T(512)S(6)} %compare.3, bf16[8,2048,2,128]{3,1,2,0:T(8,128)(2,1)} %get-tuple-element.634, s32[]{:T(128)S(6)} %select_n.78), kind=kOutput, calls=%fused_computation.29.clone.1 | convolution fusion | flops 4299161600 | bytes 52428804 | tf_op jit(solution)/shard_map/while/body/eval_jaxpr/bhqk,bqhe->bke/dot_general | solution.py:71
  1079.3 31.3 %bitcast_add_fusion.6 = f32[8,2048,128]{2,1,0:T(8,128)} fusion(f32[8,2048,128]{2,1,0:T(8,128)} %get-tuple-element.619, f32[8,512,2,2048]{3,1,2,0:T(8,128)} %fusion.134, f32[8,2,512]{2,1,0:T(2,128)S(1)} %constant_dynamic-slice_fusion.3, pred[512,2048]{1,0:T(8,128)(4,1)S(1)} %iota_compare_fusion.5, pred[]{:T(512)S(6)} %compare.3, ...), kind=kOutput, calls=%fused_computation.28.clone.1 | convolution fusion | flops 4349493248 | bytes 87064584 | tf_op jit(solution)/shard_map/while/body/eval_jaxpr/bhqk,bqhe->bke/dot_general | solution.py:66
  1125.1 16.4 copy.40
  1141.5 111.2 %all-to-all-done.3 = bf16[8,2048,2,128]{3,2,0,1:T(2,128)(2,1)} async-done(((bf16[8,2048,2,128]{3,2,0,1:T(2,128)(2,1)}), bf16[8,2048,2,128]{3,2,0,1:T(2,128)(2,1)}, u32[]{:S(2)}, u32[]{:S(2)}) %all-to-all-start.3) | async-done | bytes 8388640 | tf_op jit(solution)/shard_map/all_to_all | solution.py:101
  1258.3 23.1 %copy.47 = f32[8,8,256,2,128]{2,4,3,1,0:T(8,128)} copy(bf16[8,8,256,2,128]{4,3,0,2,1:T(2,128)(2,1)} %bitcast.60) | data formatting | bytes 25165824 | tf_op jit(solution)/shard_map/convert_element_type | solution.py:104
  1281.4 103.6 %all-to-all-done.1 = bf16[8,2048,2,128]{3,2,0,1:T(2,128)(2,1)} async-done(((bf16[8,2048,2,128]{3,2,0,1:T(2,128)(2,1)}), bf16[8,2048,2,128]{3,2,0,1:T(2,128)(2,1)}, u32[]{:S(2)}, u32[]{:S(2)}) %all-to-all-start.1) | async-done | bytes 8388640 | tf_op jit(solution)/shard_map/all_to_all | solution.py:95
  1394.1 13.8 multiply_subtract_fusion
  1407.9 22.5 %fusion.74 = f32[16,128,2048]{2,1,0:T(8,128)} fusion(bf16[8,256,16,128]{3,1,2,0:T(8,128)(2,1)S(1)} %bitcast.223, bf16[8,256,2048]{2,1,0:T(8,128)(2,1)} %param.11), kind=kOutput, calls=%fused_computation.82 | convolution fusion | flops 17179869184 | bytes 33554432 | tf_op jit(solution)/shard_map/bshe,bsd->hed/dot_general | solution.py:97
  1430.4 22.9 %fusion.71 = f32[2048,16,128]{0,2,1:T(8,128)} fusion(bf16[8,256,2048]{2,1,0:T(8,128)(2,1)S(1)} %bitcast.219, f32[8,256,16,64]{1,3,2,0:T(8,128)} %get-tuple-element.456, f32[8,256,16,64]{1,3,2,0:T(8,128)} %get-tuple-element.455), kind=kOutput, calls=%fused_computation.81 | convolution fusion | flops 17192452096 | bytes 41943040 | tf_op jit(solution)/shard_map/bsd,bshe->dhe/dot_general | solution.py:108
  1466.2 22.9 %bitcast_convert_fusion.1 = bf16[8,256,2048]{2,1,0:T(8,128)(2,1)} fusion(bf16[8,256,16,128]{3,1,2,0:T(8,128)(2,1)} %bitcast.222, bf16[16,128,2048]{2,1,0:T(8,128)(2,1)} %param.15), kind=kOutput, calls=%fused_computation.58 | convolution fusion | flops 17184063488 | bytes 25165824 | tf_op jit(solution)/shard_map/bshe,hed->bsd/dot_general | solution.py:96
  1506.1 30.7 %fusion.44 = bf16[8,256,2048]{2,1,0:T(8,128)(2,1)} fusion(f32[8,256,2048]{2,1,0:T(8,128)} %fusion.80, f32[8,256,2048]{2,1,0:T(8,128)} %fusion.83, bf16[2048,16,128]{2,1,0:T(8,128)(2,1)} %param.12, f32[8,256,16,64]{1,3,2,0:T(8,128)} %get-tuple-element.456, f32[8,256,16,64]{1,3,2,0:T(8,128)} %get-tuple-element.455), kind=kOutput, calls=%fused_computation.57 | convolution fusion | flops 17205035008 | bytes 67108864 | tf_op jit(solution)/shard_map/bshe,dhe->bsd/dot_general | solution.py:107
  1536.9 341.7 %all-reduce.3.cloned.1.call-done = (f32[2048,16,128]{0,2,1:T(8,128)}, f32[2048,128]{0,1:T(8,128)}, f32[2048,128]{0,1:T(8,128)}, f32[16,128,2048]{2,1,0:T(8,128)}) async-done(((f32[2048,16,128]{0,2,1:T(8,128)}, f32[2048,128]{0,1:T(8,128)}, f32[2048,128]{0,1:T(8,128)}, f32[16,128,2048]{2,1,0:T(8,128)}), (f32[2048,16,128]{0,2,1:T(8,128)}, f32[2048,128]{0,1:T(8,128)}, f32[2048,128]{0,1:T(8,128)}, ...) | async-done | bytes 35651600 | tf_op jit(solution)/shard_map/psum | solution.py:108
  1878.6 17.8 copy.55
  (114 shorter events, 228.6 us)
Async XLA Ops:
  7.2 1.0 copy-start
  7.2 196.7 %all-gather.3.cloned.1.call-start = ((), (), s32[]{:S(2)}) async-start(), calls=%async_computation.6 | async-start | bytes 4718592 | tf_op jit(solution)/shard_map/all_gather | solution.py:92
  8.2 41.4 %copy-start.3 = (f32[256,64]{0,1:T(8,128)}, f32[256,64]{0,1:T(8,128)S(1)}, u32[]{:S(2)}) copy-start(f32[256,64]{0,1:T(8,128)S(1)} %get-tuple-element.465) | copy-start | bytes 196612
  70.3 6.2 copy-start.8
  70.3 116.9 %all-to-all-start = ((bf16[8,256,16,128]{1,3,0,2:T(8,128)(2,1)}), bf16[8,256,16,128]{1,3,0,2:T(8,128)(2,1)}, u32[]{:S(2)}, u32[]{:S(2)}) async-start(bf16[8,256,16,128]{1,3,0,2:T(8,128)(2,1)} %copy.36), calls=%async_computation | async-start | bytes 16777216 | tf_op jit(solution)/shard_map/all_to_all | solution.py:91
  75.9 134.4 %all-gather.5.cloned.1.call-start = ((), (), s32[]{:S(2)}) async-start(), calls=%async_computation.7 | async-start | bytes 4718592 | tf_op jit(solution)/shard_map/all_gather | solution.py:93
  187.3 331.2 %all-to-all-start.2 = ((bf16[8,256,16,128]{3,1,0,2:T(8,128)(2,1)}), bf16[8,256,16,128]{3,1,0,2:T(8,128)(2,1)}, u32[]{:S(2)}, u32[]{:S(2)}) async-start(bf16[8,256,16,128]{3,1,0,2:T(8,128)(2,1)} %copy.42), calls=%async_computation.2 | async-start | bytes 16777216 | tf_op jit(solution)/shard_map/all_to_all | solution.py:99
  192.2 1261.0 %reduce-scatter.3.cloned.1.call-start = ((), (), s32[]{:S(2)}) async-start(), calls=%async_computation.8 | async-start | bytes 9437184 | tf_op jit(solution)/shard_map/reduce_scatter | solution.py:102
  1120.1 132.6 %all-to-all-start.3 = ((bf16[8,2048,2,128]{3,2,0,1:T(2,128)(2,1)}), bf16[8,2048,2,128]{3,2,0,1:T(2,128)(2,1)}, u32[]{:S(2)}, u32[]{:S(2)}) async-start(bf16[8,2048,2,128]{3,2,0,1:T(2,128)(2,1)} %get-tuple-element.319), calls=%async_computation.3 | async-start | bytes 16777216 | tf_op jit(solution)/shard_map/all_to_all | solution.py:101
  1252.7 132.3 %all-to-all-start.1 = ((bf16[8,2048,2,128]{3,2,0,1:T(2,128)(2,1)}), bf16[8,2048,2,128]{3,2,0,1:T(2,128)(2,1)}, u32[]{:S(2)}, u32[]{:S(2)}) async-start(bf16[8,2048,2,128]{3,2,0,1:T(2,128)(2,1)} %copy.40), calls=%async_computation.1 | async-start | bytes 16777216 | tf_op jit(solution)/shard_map/all_to_all | solution.py:95
  1257.7 202.6 %reduce-scatter.5.cloned.1.call-start = ((), (), s32[]{:S(2)}) async-start(), calls=%async_computation.9 | async-start | bytes 9437184 | tf_op jit(solution)/shard_map/reduce_scatter | solution.py:103
  1258.2 620.3 %all-reduce.3.cloned.1.call-start = ((), (), s32[]{:S(2)}) async-start(), calls=%async_computation.10 | async-start | bytes 71303168 | tf_op jit(solution)/shard_map/psum | solution.py:108
  1385.0 9.0 copy-start.4
  1385.0 9.0 copy-start.7
  1394.1 13.8 copy-start.2
  1394.1 36.3 %slice-start = ((s8[8388608]{0:T(1024)(128)(4,1)}), s8[4194304]{0:T(1024)(128)(4,1)S(1)}, s32[]{:S(2)}) async-start(s8[8388608]{0:T(1024)(128)(4,1)} %bitcast.218), calls=%async_computation.11 | async-start | bytes 8388608
  1407.9 22.5 %slice-start.1 = ((s8[8388608]{0:T(1024)(128)(4,1)}), s8[4194304]{0:T(1024)(128)(4,1)S(1)}, s32[]{:S(2)}) async-start(s8[8388608]{0:T(1024)(128)(4,1)} %bitcast.218), calls=%async_computation.12 | async-start | bytes 8388608
  1489.1 8.5 copy-start.1
  1489.1 8.5 copy-start.9
  1878.6 17.8 copy-start.6
  1878.6 19.1 copy-start.5
Sparse Core Ops, SparseCore 0:
  15.7 36.1 all-gather.2
  83.2 71.5 all-gather.4
  1120.2 129.9 reduce-scatter.2
  1262.2 124.0 reduce-scatter.4
  1466.4 412.1 all-reduce.2
where the time goes:
time: 1930 us; the launch traced here: 1920 us
  matrix products  929 us (48%)
  waiting for transfers between devices  631 us (33%)
  local copies, waits for them, and re-layouts  170 us (9%)
  other arithmetic  151 us (8%)
  starting transfers between devices  21.5 us (1%)
    psum x1, waiting for transfers between devices, local_step(): lax.psum(jnp.einsum('bsd,bshe->dhe', hid_loc, dq_raw, preferred_element_t...  342 us
    dot_general x4, matrix products, bwd_block(): jnp.einsum('bqhe,bke->bhqk', do_blk, v_all, preferred_element_type=jnp.fl...  157 us
    dot_general x4, matrix products, bwd_block(): jnp.einsum('bhqk,bqhe->bke', attn_probs.astype(jnp.bfloat16), do_blk, pre...  124 us
    dot_general x4, matrix products, fwd_block(): jnp.einsum('bhqk,bke->bqhe', attn_probs, v_all, preferred_element_type=jn...  111 us
    all_to_all x1, waiting for transfers between devices, local_step(): dq_pos = lax.all_to_all(dq_heads, 'sp', 1, 2, tiled=True)  111 us
    dot_general x4, matrix products, bwd_block(): jnp.einsum('bqhe,bke->bhqk', q_blk, k_all, preferred_element_type=jnp.flo...  107 us
    all_to_all x1, waiting for transfers between devices, local_step(): o_pos = lax.all_to_all(o_heads, 'sp', 1, 2, tiled=True)  104 us
    dot_general x4, matrix products, fwd_block(): jnp.einsum('bqhe,bke->bhqk', q_blk, k_all, preferred_element_type=jnp.flo...  103 us
  transfers between devices with their start and end apart: 9, of which 4 were waited for; matrix products, arithmetic and copies ran while one was open for 31% of the time, Pallas kernels for 0%

commit v1 on v0

v1 whole, which is shorter than its diff:
```python
import functools

import jax
import jax.numpy as jnp
from jax import lax
from jax.experimental import pallas as pl
from jax.experimental.pallas import tpu as pltpu
from jax.sharding import PartitionSpec as P

ROPE_BASE = 10000.0
NEG_BIG = -1e30
HEADS_PER_GROUP = 4
NT = (((1,), (1,)), ((), ()))
NN = (((1,), (0,)), ((), ()))


def dot(a, b, dims):
    return lax.dot_general(a, b, dims, preferred_element_type=jnp.float32)


def rope_tables(positions, head_dim):
    half_dim = head_dim // 2
    inv_freq = ROPE_BASE ** (-jnp.arange(half_dim, dtype=jnp.float32) * (2.0 / head_dim))
    angles = positions.astype(jnp.float32)[:, None] * inv_freq[None, :]
    cos_t, sin_t = jnp.cos(angles), jnp.sin(angles)
    return jnp.concatenate([cos_t, cos_t], -1), jnp.concatenate([-sin_t, sin_t], -1)


def swap_halves(x):
    half = x.shape[-1] // 2
    return jnp.concatenate([x[..., half:], x[..., :half]], axis=-1)


def attn_kernel(heads, first, blk_ref, q_ref, do_ref, kv_ref, kvt_ref, cos_ref, sin_ref, *rest):
    if first:
        o_ref, dq_ref, dkv_ref, q_s, do_s, s_s, ot_s, dqt_s, p_s, ds_s, dp_s = rest
    else:
        dkv_in_ref, o_ref, dq_ref, dkv_ref, q_s, do_s, s_s, ot_s, dqt_s, p_s, ds_s, dp_s = rest
    me = blk_ref[0]
    rows, hd = cos_ref.shape
    n_blk = kv_ref.shape[0]
    keys = kv_ref.shape[2]
    width = heads * rows
    scale = hd ** -0.5
    cos2, sin2 = cos_ref[...], sin_ref[...]
    do_t = []
    for h in range(heads):
        q_h = q_ref[0, :, h * hd:(h + 1) * hd].astype(jnp.float32) * scale
        q_s[h * rows:(h + 1) * rows, :] = (q_h * cos2 + swap_halves(q_h) * sin2).astype(jnp.bfloat16)
        do_s[h * rows:(h + 1) * rows, :] = do_ref[0, :, h * hd:(h + 1) * hd]

    def score_block(kb, mask, m8):
        k_blk = kv_ref[kb, 0, :, :hd]
        out = []
        for h in range(heads):
            s = dot(k_blk, q_s[h * rows:(h + 1) * rows, :], NT)
            if mask is not None:
                s = jnp.where(mask, s, NEG_BIG)
            s_s[kb, :, h * rows:(h + 1) * rows] = s
            out.append(jnp.max(s.reshape(keys // 8, 8, rows), axis=0))
        return jnp.maximum(m8, jnp.concatenate(out, axis=1))

    m8 = lax.fori_loop(0, me, lambda kb, m: score_block(kb, None, m), jnp.full((8, width), NEG_BIG, jnp.float32))
    causal = lax.broadcasted_iota(jnp.int32, (keys, rows), 0) <= lax.broadcasted_iota(jnp.int32, (keys, rows), 1)
    m8 = score_block(me, causal, m8)
    m = jnp.max(m8, axis=0, keepdims=True)

    ot_s[...] = jnp.zeros_like(ot_s)
    dqt_s[...] = jnp.zeros_like(dqt_s)

    def weigh_values(kb):
        vt = kvt_ref[kb, 0, hd:, :]
        for h in range(heads):
            cols = slice(h * rows, (h + 1) * rows)
            ot_s[:, cols] += dot(vt, p_s[:, cols], NN)

    def value_block(kb, l8):
        weigh_values(jnp.maximum(kb - 1, 0))
        out = []
        for h in range(heads):
            cols = slice(h * rows, (h + 1) * rows)
            e = jnp.exp(s_s[kb, :, cols] - m[:, cols])
            s_s[kb, :, cols] = e
            out.append(jnp.sum(e.reshape(keys // 8, 8, rows), axis=0))
            p_s[:, cols] = e.astype(jnp.bfloat16)
        return l8 + jnp.concatenate(out, axis=1)

    p_s[...] = jnp.zeros_like(p_s)
    ds_s[...] = jnp.zeros_like(ds_s)
    l8 = lax.fori_loop(0, me + 1, value_block, jnp.zeros((8, width), jnp.float32))
    weigh_values(me)
    p_s[...] = jnp.zeros_like(p_s)
    rl = 1.0 / jnp.sum(l8, axis=0, keepdims=True)
    row_dot = []
    for h in range(heads):
        cols = slice(h * rows, (h + 1) * rows)
        o_t = (ot_s[:, cols] * rl[:, cols]).astype(jnp.bfloat16)
        o_ref[0, :, h * hd:(h + 1) * hd] = o_t.T
        do_t = do_ref[0, :, h * hd:(h + 1) * hd].T
        row_dot.append(jnp.sum(do_t.astype(jnp.float32) * o_t.astype(jnp.float32), axis=0, keepdims=True))
    row_dot = jnp.concatenate(row_dot, axis=1)

    def prob_grads(kb):
        v_blk = kv_ref[kb, 0, :, hd:]
        for h in range(heads):
            cols = slice(h * rows, (h + 1) * rows)
            dp_s[:, cols] = dot(v_blk, do_s[cols, :], NT)

    def products(kb):
        kt = kvt_ref[kb, 0, :hd, :]
        for h in range(heads):
            cols = slice(h * rows, (h + 1) * rows)
            dqt_s[:, cols] += dot(kt, ds_s[:, cols], NN)
        dkv = jnp.concatenate([dot(ds_s[...], q_s[...], NN), dot(p_s[...], do_s[...], NN)], axis=1)
        if not first:
            dkv = dkv + dkv_in_ref[kb, 0]
        dkv_ref[kb, 0] = dkv

    def grad_block(kb, _):
        products(jnp.maximum(kb - 1, 0))
        for h in range(heads):
            cols = slice(h * rows, (h + 1) * rows)
            p = s_s[kb, :, cols] * rl[:, cols]
            ds_s[:, cols] = (p * (dp_s[:, cols] - row_dot[:, cols])).astype(jnp.bfloat16)
            p_s[:, cols] = p.astype(jnp.bfloat16)
        prob_grads(jnp.minimum(kb + 1, me))
        return 0

    prob_grads(0)
    lax.fori_loop(0, me + 1, grad_block, 0)
    products(me)

    def zero_block(kb, _):
        dkv_ref[kb, 0] = jnp.zeros((keys, 2 * hd), jnp.float32)
        return 0

    lax.fori_loop(me + 1, n_blk, zero_block, 0)
    for h in range(heads):
        cols = slice(h * rows, (h + 1) * rows)
        g = dqt_s[:, cols].T
        dq_ref[0, :, h * hd:(h + 1) * hd] = ((g * cos2 - swap_halves(g) * sin2) * scale).astype(jnp.bfloat16)


def attend(group, heads, me, q, do, kv, kvt, cos2, sin2, dkv):
    n_batch, rows, _ = q.shape
    n_blk, _, keys, two_hd = kv.shape
    hd = two_hd // 2
    first = dkv is None
    width = heads * hd
    head_spec = pl.BlockSpec((1, rows, width), lambda b, s: (b, 0, group))
    kv_spec = pl.BlockSpec((n_blk, 1, keys, two_hd), lambda b, s: (0, b, 0, 0))
    kvt_spec = pl.BlockSpec((n_blk, 1, two_hd, keys), lambda b, s: (0, b, 0, 0))
    tab_spec = pl.BlockSpec((rows, hd), lambda b, s: (0, 0))
    out_spec = pl.BlockSpec((1, rows, width), lambda b, s: (b, 0, 0))
    in_specs = [head_spec, head_spec, kv_spec, kvt_spec, tab_spec, tab_spec]
    operands = [me, q, do, kv, kvt, cos2, sin2]
    aliases = {}
    if not first:
        in_specs.append(kv_spec)
        operands.append(dkv)
        aliases = {7: 2}
    flops = 12 * n_batch * heads * rows * keys * n_blk * hd
    return pl.pallas_call(
        functools.partial(attn_kernel, heads, first),
        grid_spec=pltpu.PrefetchScalarGridSpec(
            num_scalar_prefetch=1,
            grid=(n_batch,),
            in_specs=in_specs,
            out_specs=[out_spec, out_spec, kv_spec],
            scratch_shapes=[
                pltpu.VMEM((heads * rows, hd), jnp.bfloat16),
                pltpu.VMEM((heads * rows, hd), jnp.bfloat16),
                pltpu.VMEM((n_blk, keys, heads * rows), jnp.float32),
                pltpu.VMEM((hd, heads * rows), jnp.float32),
                pltpu.VMEM((hd, heads * rows), jnp.float32),
                pltpu.VMEM((keys, heads * rows), jnp.bfloat16),
                pltpu.VMEM((keys, heads * rows), jnp.bfloat16),
                pltpu.VMEM((keys, heads * rows), jnp.float32),
            ],
        ),
        out_shape=[
            jax.ShapeDtypeStruct((n_batch, rows, width), jnp.bfloat16),
            jax.ShapeDtypeStruct((n_batch, rows, width), jnp.bfloat16),
            jax.ShapeDtypeStruct((n_blk, n_batch, keys, two_hd), jnp.float32),
        ],
        input_output_aliases=aliases,
        compiler_params=pltpu.CompilerParams(vmem_limit_bytes=48 * 1024 * 1024),
        cost_estimate=pl.CostEstimate(flops=2 * flops, bytes_accessed=40_000_000, transcendentals=n_batch * heads * rows * keys * n_blk),
    )(*operands)


def solution(mesh):
    n_sp = mesh.shape['sp']

    def local_step(hid_loc, gout_loc, w_query, w_key, w_value, w_out):
        n_batch, seq_loc, d_model = hid_loc.shape
        n_heads, head_dim = w_query.shape[1:]
        full = n_heads * head_dim
        n_rows = n_batch * seq_loc
        me = lax.axis_index('sp')
        cos2, sin2 = rope_tables(me * seq_loc + jnp.arange(seq_loc), head_dim)
        w_kv = jnp.concatenate([w_key, w_value], axis=1)
        hid = hid_loc.reshape(n_rows, d_model)
        gout = gout_loc.reshape(n_rows, d_model)
        wo = w_out.reshape(full, d_model)
        kv = dot(hid, w_kv, NN).astype(jnp.bfloat16).reshape(n_batch, seq_loc, 2 * head_dim)
        k_f = kv[..., :head_dim].astype(jnp.float32)
        k_rot = (k_f * cos2 + swap_halves(k_f) * sin2).astype(jnp.bfloat16)
        kv = jnp.concatenate([k_rot, kv[..., head_dim:]], axis=-1)
        kv_all = lax.all_gather(kv, 'sp', axis=0, tiled=False)
        kvt_all = jnp.swapaxes(kv_all, 2, 3)
        wq = w_query.reshape(d_model, full)
        q = dot(hid, wq, NN).astype(jnp.bfloat16).reshape(n_batch, seq_loc, full)
        do = dot(gout, wo, NT).astype(jnp.bfloat16).reshape(n_batch, seq_loc, full)
        me_arr = me.astype(jnp.int32).reshape(1)

        heads = HEADS_PER_GROUP
        n_groups = n_heads // heads
        dkv, os, dqs, dwo, dwq = None, [], [], [], []
        base = list(range(n_sp))
        for g in range(n_groups):
            o_g, dq_g, dkv = attend(g, heads, me_arr, q, do, kv_all, kvt_all, cos2, sin2, dkv)
            o_g = o_g.reshape(n_rows, heads * head_dim)
            dq_g = dq_g.reshape(n_rows, heads * head_dim)
            os.append(o_g)
            dqs.append(dq_g)
            dwo.append(dot(o_g, gout, (((0,), (0,)), ((), ()))))
            dwq.append(dot(hid, dq_g, (((0,), (0,)), ((), ()))))
            if g < n_groups - 1:
                order = [base[g + 1:] + base[:g + 1]]
                me_arr, dwo[g], dwq[g] = lax.optimization_barrier((me_arr, dwo[g], dwq[g]))
                if g > 0:
                    me_arr, dwo[g - 1], dwq[g - 1] = lax.optimization_barrier((me_arr, dwo[g - 1], dwq[g - 1]))
                dwo[g], dwq[g] = lax.psum((dwo[g], dwq[g]), 'sp', axis_index_groups=order)
        dkv, dwo[-2], dwq[-2] = lax.optimization_barrier((dkv, dwo[-2], dwq[-2]))
        attn_out = dot(jnp.concatenate(os, axis=1), wo, NN).astype(jnp.bfloat16)
        dkv_loc = lax.psum_scatter(dkv, 'sp', scatter_dimension=0, tiled=False)
        dk_f = dkv_loc[..., :head_dim]
        dk_raw = (dk_f * cos2 - swap_halves(dk_f) * sin2).astype(jnp.bfloat16)
        dkv_raw = jnp.concatenate([dk_raw, dkv_loc[..., head_dim:].astype(jnp.bfloat16)], axis=-1).reshape(n_rows, 2 * head_dim)
        dw_kv = dot(hid, dkv_raw, (((0,), (0,)), ((), ())))
        dwo[-1], dwq[-1], dw_kv = lax.psum((dwo[-1], dwq[-1], dw_kv), 'sp')
        d_hidden = (dot(jnp.concatenate(dqs, axis=1), wq, NT) + dot(dkv_raw, w_kv, NT)).astype(jnp.bfloat16)
        dw_query = jnp.concatenate([w.reshape(d_model, heads, head_dim) for w in dwq], axis=1)
        dw_out = jnp.concatenate(dwo, axis=0).reshape(n_heads, head_dim, d_model)
        return (attn_out.reshape(hid_loc.shape), d_hidden.reshape(hid_loc.shape), dw_query, dw_kv[:, :head_dim], dw_kv[:, head_dim:], dw_out)

    act_spec = P('dp', 'sp', None)
    return jax.shard_map(local_step, mesh=mesh, in_specs=(act_spec, act_spec, P(), P(), P(), P()), out_specs=(act_spec, act_spec, P('dp', None, None), P('dp', None), P('dp', None), P('dp', None, None)), check_vma=False)
```

time: 1930 us -> 874 us (0.45)
  matrix products: 929 us -> 197 us
  waiting for transfers between devices: 631 us -> 468 us
  other arithmetic: 151 us -> 25.7 us
  local copies, waits for them, and re-layouts: 170 us -> 50.8 us
  Pallas kernels: 0 us -> 113 us
  starting transfers between devices: 21.5 us -> 0.41 us
    dot_general x40 -> x15, matrix products: 929 us -> 197 us  [dot(): return lax.dot_general(a, b, dims, preferred_element_type=jnp.float32)]
    all_to_all x4 -> x0, waiting for transfers between devices: 288 us -> none  [the longest x1 111 us: local_step(): dq_pos = lax.all_to_all(dq_heads, 'sp', 1, 2, tiled=True)]
    pallas_call x0 -> x4, Pallas kernels: none -> 113 us  [attend(): pl.pallas_call(functools.partial(attn_kernel, heads, first), grid_spec=pl...]
    reduce_sum x4 -> x0, other arithmetic: 85.8 us -> none  [fwd_block(): row_sum = jnp.sum(exp_scores, axis=-1, keepdims=True)]
    psum x1 -> x4, waiting for transfers between devices: 342 us -> 413 us  [the longest x3 306 us: local_step(): dwo[g], dwq[g] = lax.psum((dwo[g], dwq[g]), 'sp', axis_index_groups=order)]
    reduce_scatter x2 -> x1, waiting for transfers between devices: 0.02 us -> 49.2 us  [local_step(): dkv_loc = lax.psum_scatter(dkv, 'sp', scatter_dimension=0, tiled=False)]
    unnamed x30 -> x37, local copies, waits for them, and re-layouts: 51.1 us -> 10.5 us
    convert_element_type x2 -> x1, local copies, waits for them, and re-layouts: 30.9 us -> 0.52 us  [local_step(): dot(hid, w_kv, NN).astype(jnp.bfloat16)]
  transfers between devices with their start and end apart: 9 -> 6, of which waited for: 4 -> 6; matrix products, arithmetic and copies ran while one was open for 31% -> 21% of each run, Pallas kernels for 0% -> 10%
where the time goes in v1:
time: 874 us; the launch traced here: 869 us
  waiting for transfers between devices  468 us (54%)
  matrix products  197 us (23%)
  Pallas kernels  113 us (13%)
  local copies, waits for them, and re-layouts  50.8 us (6%)
  other arithmetic  25.7 us (3%)
  between operations  14.5 us (2%)
    psum x3, waiting for transfers between devices, local_step(): dwo[g], dwq[g] = lax.psum((dwo[g], dwq[g]), 'sp', axis_index_groups=order)  306 us
    dot_general x15, matrix products, dot(): return lax.dot_general(a, b, dims, preferred_element_type=jnp.float32)  197 us
    pallas_call x4, Pallas kernels, attend(): pl.pallas_call(functools.partial(attn_kernel, heads, first), grid_spec=pl...  113 us
    psum x1, waiting for transfers between devices, local_step(): dwo[-1], dwq[-1], dw_kv = lax.psum((dwo[-1], dwq[-1], dw_kv), 'sp')  107 us
    reduce_scatter x1, waiting for transfers between devices, local_step(): dkv_loc = lax.psum_scatter(dkv, 'sp', scatter_dimension=0, tiled=False)  49.2 us
    reshape x4, local copies, waits for them, and re-layouts, local_step(): w.reshape(d_model, heads, head_dim)  21.4 us
  transfers between devices with their start and end apart: 6, of which 6 were waited for; matrix products, arithmetic and copies ran while one was open for 21% of the time, Pallas kernels for 10%

profile of v1, /device:TPU:0, one launch (start us, length us, event | category | flops | bytes accessed | tf_op | source)
XLA Modules:
  0.0 869.1 jit_solution(17301586624241376461)
XLA Ops:
  7.2 1.1 constant_dynamic-update-slice_fusion.1
  8.4 1.2 constant_dynamic-update-slice_fusion
  9.6 1.0 copy-done.15
  10.5 5.8 fusion.26
  17.4 0.5 multiply_cosine_fusion
  18.5 1.1 pad_maximum_fusion.2
  19.8 23.7 %convolution_convert_fusion = bf16[2048,2048]{1,0:T(8,128)(2,1)} fusion(bf16[2048,2048]{1,0:T(8,128)(2,1)} %bitcast.123, bf16[2048,2048]{1,0:T(8,128)(2,1)} %bitcast.124), kind=kOutput, calls=%fused_computation.23 | convolution fusion | flops 17184063488 | bytes 25165824 | tf_op jit(solution)/shard_map/dot_general | solution.py:18
  43.5 23.4 %fusion.21 = bf16[2048,2048]{1,0:T(8,128)(2,1)} fusion(bf16[2048,2048]{1,0:T(8,128)(2,1)} %bitcast.104, bf16[256,8,16,128]{3,2,1,0:T(8,128)(2,1)} %bitcast.126), kind=kOutput, calls=%fused_computation.22 | convolution fusion | flops 17184063488 | bytes 25165824 | tf_op jit(solution)/shard_map/dot_general | solution.py:18
  66.9 5.9 all-gather.3.cloned.1.call-done
  72.7 11.9 %copy.37 = bf16[64,256,256]{1,2,0:T(8,128)(2,1)} copy(bf16[64,256,256]{2,1,0:T(8,128)(2,1)} %all-gather.3.cloned.1.call-done) | data formatting | bytes 16777216 | tf_op jit(solution)/shard_map/all_gather | solution.py:210
  84.6 27.4 %shard_map.109 = (bf16[8,256,512]{2,1,0:T(8,128)(2,1)S(1)}, bf16[8,256,512]{2,1,0:T(8,128)(2,1)S(1)}, f32[8,8,256,256]{3,2,1,0:T(8,128)}) custom-call(s32[1]{0:T(128)} %bitcast.blk_ref, bf16[8,256,2048]{2,1,0:T(8,128)(2,1)} %bitcast.132, bf16[8,256,2048]{2,1,0:T(8,128)(2,1)} %bitcast.128, bf16[8,8,256,256]{3,2,1,0:T(8,128)(2,1)} %bitcast.105, ...), custom_call_target="tpu_custom_call" | custom-call | flops 51539607552 | bytes 40000000 | tf_op jit(solution)/shard_map/pallas_call | solution.py:163
  112.0 11.0 %convolution_bitcast_fusion.6 = f32[512,2048]{1,0:T(8,128)} fusion(bf16[8,256,512]{2,1,0:T(8,128)(2,1)S(1)} %get-tuple-element.36, bf16[8,256,2048]{2,1,0:T(8,128)(2,1)} %param.7), kind=kOutput, calls=%fused_computation.32 | convolution fusion | flops 4294967296 | bytes 14680064 | tf_op jit(solution)/shard_map/dot_general | solution.py:18
  123.0 9.4 %convolution_bitcast_fusion.5 = f32[2048,512]{0,1:T(8,128)} fusion(bf16[8,256,512]{2,1,0:T(8,128)(2,1)S(1)} %get-tuple-element.37, bf16[8,256,2048]{2,1,0:T(8,128)(2,1)} %param.6), kind=kOutput, calls=%fused_computation.31 | convolution fusion | flops 4294967296 | bytes 14680064 | tf_op jit(solution)/shard_map/dot_general | solution.py:18
  132.5 28.4 %shard_map.110 = (bf16[8,256,512]{2,1,0:T(8,128)(2,1)S(1)}, bf16[8,256,512]{2,1,0:T(8,128)(2,1)S(1)}, f32[8,8,256,256]{3,2,1,0:T(8,128)}) custom-call(s32[1]{0:T(128)} %bitcast.blk_ref, bf16[8,256,2048]{2,1,0:T(8,128)(2,1)} %bitcast.133, bf16[8,256,2048]{2,1,0:T(8,128)(2,1)} %bitcast.129, ...), custom_call_target="tpu_custom_call", output_to_operand_aliasing={{2}: (7, {})} | custom-call | flops 51539607552 | bytes 40000000 | tf_op jit(solution)/shard_map/pallas_call | solution.py:163
  160.9 10.2 %convolution_bitcast_fusion.4 = f32[512,2048]{1,0:T(8,128)} fusion(bf16[8,256,512]{2,1,0:T(8,128)(2,1)S(1)} %get-tuple-element.40, bf16[8,256,2048]{2,1,0:T(8,128)(2,1)} %param.7), kind=kOutput, calls=%fused_computation.30 | convolution fusion | flops 4294967296 | bytes 14680064 | tf_op jit(solution)/shard_map/dot_general | solution.py:18
  171.0 9.5 %convolution_bitcast_fusion.3 = f32[2048,512]{0,1:T(8,128)} fusion(bf16[8,256,512]{2,1,0:T(8,128)(2,1)S(1)} %get-tuple-element.41, bf16[8,256,2048]{2,1,0:T(8,128)(2,1)} %param.6), kind=kOutput, calls=%fused_computation.29 | convolution fusion | flops 4294967296 | bytes 14680064 | tf_op jit(solution)/shard_map/dot_general | solution.py:18
  180.6 142.2 %all-reduce.11.cloned.1.call-done = (f32[512,2048]{1,0:T(8,128)}, f32[2048,512]{0,1:T(8,128)}) async-done(((f32[512,2048]{1,0:T(8,128)}, f32[2048,512]{0,1:T(8,128)}), (f32[512,2048]{1,0:T(8,128)}, f32[2048,512]{0,1:T(8,128)})) %all-reduce.11.cloned.1.call-update) | async-done | bytes 8388624 | tf_op jit(solution)/shard_map/psum | solution.py:234
  322.7 28.7 %shard_map.111 = (bf16[8,256,512]{2,1,0:T(8,128)(2,1)S(1)}, bf16[8,256,512]{2,1,0:T(8,128)(2,1)S(1)}, f32[8,8,256,256]{3,2,1,0:T(8,128)}) custom-call(s32[1]{0:T(128)} %bitcast.blk_ref, bf16[8,256,2048]{2,1,0:T(8,128)(2,1)} %bitcast.134, bf16[8,256,2048]{2,1,0:T(8,128)(2,1)} %bitcast.130, ...), custom_call_target="tpu_custom_call", output_to_operand_aliasing={{2}: (7, {})} | custom-call | flops 51539607552 | bytes 40000000 | tf_op jit(solution)/shard_map/pallas_call | solution.py:163
  351.5 11.0 %convolution_bitcast_fusion.2 = f32[512,2048]{1,0:T(8,128)} fusion(bf16[8,256,512]{2,1,0:T(8,128)(2,1)S(1)} %get-tuple-element.47, bf16[8,256,2048]{2,1,0:T(8,128)(2,1)} %param.7), kind=kOutput, calls=%fused_computation.28 | convolution fusion | flops 4294967296 | bytes 14680064 | tf_op jit(solution)/shard_map/dot_general | solution.py:18
  362.5 9.4 %convolution_bitcast_fusion.1 = f32[2048,512]{0,1:T(8,128)} fusion(bf16[8,256,512]{2,1,0:T(8,128)(2,1)S(1)} %get-tuple-element.48, bf16[8,256,2048]{2,1,0:T(8,128)(2,1)} %param.6), kind=kOutput, calls=%fused_computation.27 | convolution fusion | flops 4294967296 | bytes 14680064 | tf_op jit(solution)/shard_map/dot_general | solution.py:18
  371.9 73.0 %all-reduce.13.cloned.1.call-done = (f32[512,2048]{1,0:T(8,128)}, f32[2048,512]{0,1:T(8,128)}) async-done(((f32[512,2048]{1,0:T(8,128)}, f32[2048,512]{0,1:T(8,128)}), (f32[512,2048]{1,0:T(8,128)}, f32[2048,512]{0,1:T(8,128)})) %all-reduce.13.cloned.1.call-update) | async-done | bytes 8388624 | tf_op jit(solution)/shard_map/psum | solution.py:234
  445.0 28.4 %shard_map.112 = (bf16[8,256,512]{2,1,0:T(8,128)(2,1)S(1)}, bf16[8,256,512]{2,1,0:T(8,128)(2,1)S(1)}, f32[8,8,256,256]{3,2,1,0:T(8,128)}) custom-call(s32[1]{0:T(128)} %bitcast.blk_ref, bf16[8,256,2048]{2,1,0:T(8,128)(2,1)} %bitcast.135, bf16[8,256,2048]{2,1,0:T(8,128)(2,1)} %bitcast.131, ...), custom_call_target="tpu_custom_call", output_to_operand_aliasing={{2}: (7, {})} | custom-call | flops 51539607552 | bytes 40000000 | tf_op jit(solution)/shard_map/pallas_call | solution.py:163
  473.4 1.3 copy-done.6
  474.7 1.3 copy-done.9
  476.0 91.0 %all-reduce.15.cloned.1.call-done = (f32[512,2048]{1,0:T(8,128)}, f32[2048,512]{0,1:T(8,128)}) async-done(((f32[512,2048]{1,0:T(8,128)}, f32[2048,512]{0,1:T(8,128)}), (f32[512,2048]{1,0:T(8,128)}, f32[2048,512]{0,1:T(8,128)})) %all-reduce.15.cloned.1.call-update) | async-done | bytes 8388624 | tf_op jit(solution)/shard_map/psum | solution.py:234
  567.0 5.5 copy.50
  572.5 5.3 copy.51
  577.8 10.6 %fusion.38 = f32[512,2048,1]{1,0,2:T(8,128)} fusion(bf16[8,256,512]{2,1,0:T(8,128)(2,1)} %copy-done.6, bf16[8,256,2048]{2,1,0:T(8,128)(2,1)} %param.6), kind=kOutput, calls=%fused_computation.62 | convolution fusion | flops 4294967296 | bytes 14680064 | tf_op jit(solution)/shard_map/dot_general | solution.py:18
  588.4 5.2 copy.49
  593.6 10.8 %convolution_bitcast_fusion = f32[512,2048]{1,0:T(8,128)} fusion(bf16[8,256,512]{2,1,0:T(8,128)(2,1)} %copy-done.9, bf16[8,256,2048]{2,1,0:T(8,128)(2,1)} %param.7), kind=kOutput, calls=%fused_computation.26 | convolution fusion | flops 4294967296 | bytes 14680064 | tf_op jit(solution)/shard_map/dot_general | solution.py:18
  604.4 21.6 %fusion.18 = bf16[2048,2048]{1,0:T(8,128)(2,1)} fusion(bf16[2048,2048]{1,0:T(8,128)(2,1)} %bitcast.125, bf16[2048,512]{1,0:T(8,128)(2,1)S(1)} %bitcast.101, bf16[2048,512]{1,0:T(8,128)(2,1)S(1)} %bitcast.100, bf16[2048,512]{1,0:T(8,128)(2,1)S(1)} %bitcast.98, bf16[2048,512]{1,0:T(8,128)(2,1)S(1)} %bitcast.96), kind=kOutput, calls=%fused_computation.21 | convolution fusion | flops 17217617920 | bytes 25165824 | tf_op jit(solution)/shard_map/dot_general | solution.py:18
  626.1 5.4 copy.52
  631.5 49.2 %reduce-scatter.2.cloned.1.call-done = f32[1,8,256,256]{3,2,1,0:T(8,128)} async-done(((f32[8,8,256,256]{3,2,1,0:T(8,128)}), f32[1,8,256,256]{3,2,1,0:T(8,128)}) %reduce-scatter.2.cloned.1.call-update) | async-done | bytes 2097168 | tf_op jit(solution)/shard_map/reduce_scatter | solution.py:237
  680.7 1.3 slice.62
  682.0 2.0 fusion.35
  683.9 1.6 fusion.28
  685.6 7.1 convolution_bitcast_fusion.7
  692.8 1.1 copy-done.16
  693.9 8.5 fusion.37
  702.4 25.0 %add_convert_fusion = bf16[2048,2048]{1,0:T(8,128)(2,1)} fusion(f32[2048,2048]{1,0:T(8,128)} %fusion.37, bf16[2048,512]{1,0:T(8,128)(2,1)} %bitcast.99, bf16[2048,512]{1,0:T(8,128)(2,1)} %bitcast.97, bf16[2048,512]{1,0:T(8,128)(2,1)} %bitcast.95, bf16[2048,512]{1,0:T(8,128)(2,1)S(1)} %bitcast.94, bf16[256,8,16,128]{3,2,1,0:T(8,128)(2,1)} %bitcast.127), kind=kOutput, calls=%fused_computation.2 | convolution fusion | flops 17221812224 | bytes 41943040 | tf_op jit(solution)/shard_map/dot_general | solution.py:18
  727.5 106.6 %all-reduce.9.cloned.1.call-done = (f32[2048,4,128]{2,1,0:T(4,128)}, f32[2048,256]{0,1:T(8,128)}, f32[512,2048]{1,0:T(8,128)}) async-done(((f32[2048,4,128]{2,1,0:T(4,128)}, f32[2048,256]{0,1:T(8,128)}, f32[512,2048]{1,0:T(8,128)}), (f32[2048,4,128]{2,1,0:T(4,128)}, f32[2048,256]{0,1:T(8,128)}, f32[512,2048]{1,0:T(8,128)})) %all-reduce.9.cloned.1.call-update) | async-done | bytes 10485776 | tf_op jit(solution)/shard_map/psum | solution.py:242
  834.0 1.7 fusion.34
  835.7 1.3 copy.56
  837.0 1.3 copy.55
  838.3 14.5 %pad_maximum_fusion = f32[2048,16,128]{2,1,0:T(8,128)} fusion(f32[2048,4,128]{2,1,0:T(4,128)} %get-tuple-element.78, f32[2048,4,128]{2,1,0:T(4,128)} %copy.52, f32[2048,4,128]{2,1,0:T(4,128)} %copy.51, f32[2048,4,128]{2,1,0:T(4,128)} %copy.50), kind=kLoop, calls=%fused_computation | loop fusion | flops 12582912 | bytes 33554432 | tf_op jit(solution)/shard_map/concatenate | solution.py:244
  852.9 0.6 copy-done.13
  853.5 1.5 copy-done.14
  854.9 7.1 pad_maximum_fusion.1
  (48 shorter events, 2.3 us)
Async XLA Ops:
  7.2 65.6 %all-gather.3.cloned.1.call-start = ((), (), s32[]{:S(2)}) async-start(), calls=%async_computation.2 | async-start | bytes 9437184 | tf_op jit(solution)/shard_map/all_gather | solution.py:210
  9.6 1.0 copy-start.15
  19.6 303.1 %all-reduce.11.cloned.1.call-start = ((), (), s32[]{:S(2)}) async-start(), calls=%async_computation.4 | async-start | bytes 16777216 | tf_op jit(solution)/shard_map/psum | solution.py:234
  112.0 11.0 %copy-start.3 = (bf16[8,256,512]{2,1,0:T(8,128)(2,1)}, bf16[8,256,512]{2,1,0:T(8,128)(2,1)S(1)}, u32[]{:S(2)}) copy-start(bf16[8,256,512]{2,1,0:T(8,128)(2,1)S(1)} %get-tuple-element.36) | copy-start | bytes 6291460
  112.0 11.0 %copy-start = (bf16[8,256,512]{2,1,0:T(8,128)(2,1)}, bf16[8,256,512]{2,1,0:T(8,128)(2,1)S(1)}, u32[]{:S(2)}) copy-start(bf16[8,256,512]{2,1,0:T(8,128)(2,1)S(1)} %get-tuple-element.37) | copy-start | bytes 6291460
  132.5 312.5 %all-reduce.13.cloned.1.call-start = ((), (), s32[]{:S(2)}) async-start(), calls=%async_computation.5 | async-start | bytes 16777216 | tf_op jit(solution)/shard_map/psum | solution.py:234
  160.9 10.2 %copy-start.2 = (bf16[8,256,512]{2,1,0:T(8,128)(2,1)}, bf16[8,256,512]{2,1,0:T(8,128)(2,1)S(1)}, u32[]{:S(2)}) copy-start(bf16[8,256,512]{2,1,0:T(8,128)(2,1)S(1)} %get-tuple-element.41) | copy-start | bytes 6291460
  180.5 386.4 %all-reduce.15.cloned.1.call-start = ((), (), s32[]{:S(2)}) async-start(), calls=%async_computation.6 | async-start | bytes 16777216 | tf_op jit(solution)/shard_map/psum | solution.py:234
  351.5 11.0 %copy-start.7 = (bf16[8,256,512]{2,1,0:T(8,128)(2,1)}, bf16[8,256,512]{2,1,0:T(8,128)(2,1)S(1)}, u32[]{:S(2)}) copy-start(bf16[8,256,512]{2,1,0:T(8,128)(2,1)S(1)} %get-tuple-element.47) | copy-start | bytes 6291460
  351.5 11.0 %copy-start.5 = (bf16[8,256,512]{2,1,0:T(8,128)(2,1)}, bf16[8,256,512]{2,1,0:T(8,128)(2,1)S(1)}, u32[]{:S(2)}) copy-start(bf16[8,256,512]{2,1,0:T(8,128)(2,1)S(1)} %get-tuple-element.48) | copy-start | bytes 6291460
  444.9 235.7 %reduce-scatter.2.cloned.1.call-start = ((), (), s32[]{:S(2)}) async-start(), calls=%async_computation.1 | async-start | bytes 18874368 | tf_op jit(solution)/shard_map/reduce_scatter | solution.py:237
  473.4 1.3 copy-start.6
  474.7 1.3 copy-start.9
  567.0 267.1 %all-reduce.9.cloned.1.call-start = ((), (), s32[]{:S(2)}) async-start(), calls=%async_computation.3 | async-start | bytes 20971520 | tf_op jit(solution)/shard_map/psum | solution.py:242
  593.6 10.8 %copy-start.4 = (bf16[8,256,512]{2,1,0:T(8,128)(2,1)S(1)}, bf16[8,256,512]{2,1,0:T(8,128)(2,1)}, u32[]{:S(2)}) copy-start(bf16[8,256,512]{2,1,0:T(8,128)(2,1)} %copy-done.3) | copy-start | bytes 6291460
  593.6 10.8 %copy-start.8 = (bf16[8,256,512]{2,1,0:T(8,128)(2,1)S(1)}, bf16[8,256,512]{2,1,0:T(8,128)(2,1)}, u32[]{:S(2)}) copy-start(bf16[8,256,512]{2,1,0:T(8,128)(2,1)} %copy-done.7) | copy-start | bytes 6291460
  593.6 10.8 %copy-start.10 = (bf16[8,256,512]{2,1,0:T(8,128)(2,1)S(1)}, bf16[8,256,512]{2,1,0:T(8,128)(2,1)}, u32[]{:S(2)}) copy-start(bf16[8,256,512]{2,1,0:T(8,128)(2,1)} %copy-done.9) | copy-start | bytes 6291460
  692.7 1.2 copy-start.16
  693.9 8.5 copy-start.1
  838.3 14.5 %copy-start.11 = (f32[512,2048]{1,0:T(8,128)S(1)}, f32[512,2048]{1,0:T(8,128)}, u32[]{:S(2)}) copy-start(f32[512,2048]{1,0:T(8,128)} %get-tuple-element.63) | copy-start | bytes 12582916
  838.3 14.5 %copy-start.12 = (f32[512,2048]{1,0:T(8,128)S(1)}, f32[512,2048]{1,0:T(8,128)}, u32[]{:S(2)}) copy-start(f32[512,2048]{1,0:T(8,128)} %get-tuple-element.64) | copy-start | bytes 12582916
  838.3 15.1 %copy-start.13 = (f32[512,2048]{1,0:T(8,128)S(1)}, f32[512,2048]{1,0:T(8,128)}, u32[]{:S(2)}) copy-start(f32[512,2048]{1,0:T(8,128)} %get-tuple-element.65) | copy-start | bytes 12582916
  838.3 16.6 %copy-start.14 = (f32[512,2048]{1,0:T(8,128)S(1)}, f32[512,2048]{1,0:T(8,128)}, u32[]{:S(2)}) copy-start(f32[512,2048]{1,0:T(8,128)} %get-tuple-element.80) | copy-start | bytes 12582916
Sparse Core Ops, SparseCore 0:
  19.7 52.9 all-gather.2
  132.6 190.1 all-reduce.10
  326.5 118.4 all-reduce.12
  448.5 118.4 all-reduce.14
  570.9 109.7 reduce-scatter.1
  692.8 141.1 all-reduce.8

commit v2 on v1

v2 whole, which is shorter than its diff:
```python
import functools

import jax
import jax.numpy as jnp
from jax import lax
from jax.experimental import pallas as pl
from jax.experimental.pallas import tpu as pltpu
from jax.sharding import PartitionSpec as P

ROPE_BASE = 10000.0
NEG_BIG = -1e30
HEAD_GROUPS = (6, 6, 4)
KEY_SPAN = 2
NT = (((1,), (1,)), ((), ()))
NN = (((1,), (0,)), ((), ()))


def dot(a, b, dims):
    return lax.dot_general(a, b, dims, preferred_element_type=jnp.float32)


def rope_tables(positions, head_dim):
    half_dim = head_dim // 2
    inv_freq = ROPE_BASE ** (-jnp.arange(half_dim, dtype=jnp.float32) * (2.0 / head_dim))
    angles = positions.astype(jnp.float32)[:, None] * inv_freq[None, :]
    cos_t, sin_t = jnp.cos(angles), jnp.sin(angles)
    return jnp.concatenate([cos_t, cos_t], -1), jnp.concatenate([-sin_t, sin_t], -1)


def swap_halves(x):
    half = x.shape[-1] // 2
    return jnp.concatenate([x[..., half:], x[..., :half]], axis=-1)


def attn_kernel(heads, first, last, blk_ref, q_ref, do_ref, kv_ref, cos_ref, sin_ref, *rest):
    rest = list(rest)
    dkv_in_ref = None if first else rest.pop(0)
    o_ref, dq_ref = rest.pop(0), rest.pop(0)
    dkv_refs = [rest.pop(0) for _ in range(2 if last else 1)]
    q_s, do_s, s_s, ot_s, dqt_s, p_s, ds_s, dp_s = rest
    me = blk_ref[0]
    rows, hd = cos_ref.shape
    n_blk = kv_ref.shape[0] // KEY_SPAN
    blk = kv_ref.shape[2]
    keys = KEY_SPAN * blk
    width = heads * rows
    scale = hd ** -0.5
    end = lax.div(me, KEY_SPAN)
    cos2, sin2 = cos_ref[...], sin_ref[...]
    for h in range(heads):
        q_h = q_ref[0, :, h * hd:(h + 1) * hd].astype(jnp.float32) * scale
        q_s[h * rows:(h + 1) * rows, :] = (q_h * cos2 + swap_halves(q_h) * sin2).astype(jnp.bfloat16)
        do_s[h * rows:(h + 1) * rows, :] = do_ref[0, :, h * hd:(h + 1) * hd]

    def k_span(kb):
        return kv_ref[pl.ds(kb * KEY_SPAN, KEY_SPAN), 0, :, :hd].reshape(keys, hd)

    def v_span(kb):
        return kv_ref[pl.ds(kb * KEY_SPAN, KEY_SPAN), 0, :, hd:].reshape(keys, hd)

    def score_block(kb, mask, m8):
        k_blk = k_span(kb)
        out = []
        for h in range(heads):
            s = dot(k_blk, q_s[h * rows:(h + 1) * rows, :], NT)
            if mask is not None:
                s = jnp.where(mask, s, NEG_BIG)
            s_s[kb, :, h * rows:(h + 1) * rows] = s
            out.append(jnp.max(s.reshape(keys // 8, 8, rows), axis=0))
        return jnp.maximum(m8, jnp.concatenate(out, axis=1))

    m8 = lax.fori_loop(0, end, lambda kb, m: score_block(kb, None, m), jnp.full((8, width), NEG_BIG, jnp.float32))
    key_pos = lax.broadcasted_iota(jnp.int32, (keys, rows), 0) + end * keys
    causal = key_pos <= lax.broadcasted_iota(jnp.int32, (keys, rows), 1) + me * rows
    m8 = score_block(end, causal, m8)
    m = jnp.max(m8, axis=0, keepdims=True)

    ot_s[...] = jnp.zeros_like(ot_s)
    dqt_s[...] = jnp.zeros_like(dqt_s)

    def weigh_values(kb):
        vt = v_span(kb).T
        for h in range(heads):
            cols = slice(h * rows, (h + 1) * rows)
            ot_s[:, cols] += dot(vt, p_s[:, cols], NN)

    def value_block(kb, l8):
        weigh_values(jnp.maximum(kb - 1, 0))
        out = []
        for h in range(heads):
            cols = slice(h * rows, (h + 1) * rows)
            e = jnp.exp(s_s[kb, :, cols] - m[:, cols])
            s_s[kb, :, cols] = e
            out.append(jnp.sum(e.reshape(keys // 8, 8, rows), axis=0))
            p_s[:, cols] = e.astype(jnp.bfloat16)
        return l8 + jnp.concatenate(out, axis=1)

    p_s[...] = jnp.zeros_like(p_s)
    ds_s[...] = jnp.zeros_like(ds_s)
    l8 = lax.fori_loop(0, end + 1, value_block, jnp.zeros((8, width), jnp.float32))
    weigh_values(end)
    p_s[...] = jnp.zeros_like(p_s)
    rl = 1.0 / jnp.sum(l8, axis=0, keepdims=True)
    row_dot = []
    for h in range(heads):
        cols = slice(h * rows, (h + 1) * rows)
        o_t = (ot_s[:, cols] * rl[:, cols]).astype(jnp.bfloat16)
        o_ref[0, :, h * hd:(h + 1) * hd] = o_t.T
        do_t = do_ref[0, :, h * hd:(h + 1) * hd].T
        row_dot.append(jnp.sum(do_t.astype(jnp.float32) * o_t.astype(jnp.float32), axis=0, keepdims=True))
    row_dot = jnp.concatenate(row_dot, axis=1)

    def prob_grads(kb):
        v_blk = v_span(kb)
        for h in range(heads):
            cols = slice(h * rows, (h + 1) * rows)
            dp_s[:, cols] = dot(v_blk, do_s[cols, :], NT)

    def put_dkv(kb, dkv):
        dkv = dkv.reshape(KEY_SPAN, blk, 2 * hd)
        if not first:
            dkv = dkv + dkv_in_ref[pl.ds(kb * KEY_SPAN, KEY_SPAN), 0]
        if last:
            odd = lax.rem(me, 2) == 1
            dkv_refs[0][kb, 0] = jnp.where(odd, dkv[1], dkv[0]).astype(jnp.bfloat16)
            dkv_refs[1][kb, 0] = jnp.where(odd, dkv[0], dkv[1]).astype(jnp.bfloat16)
        else:
            dkv_refs[0][pl.ds(kb * KEY_SPAN, KEY_SPAN), 0] = dkv

    def products(kb):
        kt = k_span(kb).T
        for h in range(heads):
            cols = slice(h * rows, (h + 1) * rows)
            dqt_s[:, cols] += dot(kt, ds_s[:, cols], NN)
        put_dkv(kb, jnp.concatenate([dot(ds_s[...], q_s[...], NN), dot(p_s[...], do_s[...], NN)], axis=1))

    def grad_block(kb, _):
        products(jnp.maximum(kb - 1, 0))
        for h in range(heads):
            cols = slice(h * rows, (h + 1) * rows)
            p = s_s[kb, :, cols] * rl[:, cols]
            ds_s[:, cols] = (p * (dp_s[:, cols] - row_dot[:, cols])).astype(jnp.bfloat16)
            p_s[:, cols] = p.astype(jnp.bfloat16)
        prob_grads(jnp.minimum(kb + 1, end))
        return 0

    prob_grads(0)
    lax.fori_loop(0, end + 1, grad_block, 0)
    products(end)

    def zero_block(kb, _):
        for ref in dkv_refs:
            n = ref.shape[0] // n_blk
            ref[pl.ds(kb * n, n)] = jnp.zeros((n, 1, blk, 2 * hd), ref.dtype)
        return 0

    lax.fori_loop(end + 1, n_blk, zero_block, 0)
    for h in range(heads):
        cols = slice(h * rows, (h + 1) * rows)
        g = dqt_s[:, cols].T
        dq_ref[0, :, h * hd:(h + 1) * hd] = ((g * cos2 - swap_halves(g) * sin2) * scale).astype(jnp.bfloat16)


def attend(group, heads, me, q, do, kv, cos2, sin2, dkv, last=False):
    n_batch, rows, _ = q.shape
    n_blk, _, blk, two_hd = kv.shape
    hd = two_hd // 2
    first = dkv is None
    width = heads * hd
    keys = KEY_SPAN * blk
    head_spec = pl.BlockSpec((1, rows, width), lambda b, s: (b, 0, group))
    kv_spec = pl.BlockSpec((n_blk, 1, blk, two_hd), lambda b, s: (0, b, 0, 0))
    half_spec = pl.BlockSpec((n_blk // 2, 1, blk, two_hd), lambda b, s: (0, b, 0, 0))
    tab_spec = pl.BlockSpec((rows, hd), lambda b, s: (0, 0))
    out_spec = pl.BlockSpec((1, rows, width), lambda b, s: (b, 0, 0))
    in_specs = [head_spec, head_spec, kv_spec, tab_spec, tab_spec]
    operands = [me, q, do, kv, cos2, sin2]
    aliases = {}
    if not first:
        in_specs.append(kv_spec)
        operands.append(dkv)
        if not last:
            aliases = {6: 2}
    head_shape = jax.ShapeDtypeStruct((n_batch, rows, width), jnp.bfloat16)
    if last:
        dkv_specs = [half_spec] * 2
        dkv_shapes = [jax.ShapeDtypeStruct((n_blk // 2, n_batch, blk, two_hd), jnp.bfloat16)] * 2
    else:
        dkv_specs = [kv_spec]
        dkv_shapes = [jax.ShapeDtypeStruct((n_blk, n_batch, blk, two_hd), jnp.float32)]
    scores = n_batch * heads * rows * blk * n_blk
    return pl.pallas_call(
        functools.partial(attn_kernel, heads, first, last),
        grid_spec=pltpu.PrefetchScalarGridSpec(
            num_scalar_prefetch=1,
            grid=(n_batch,),
            in_specs=in_specs,
            out_specs=[out_spec, out_spec] + dkv_specs,
            scratch_shapes=[
                pltpu.VMEM((heads * rows, hd), jnp.bfloat16),
                pltpu.VMEM((heads * rows, hd), jnp.bfloat16),
                pltpu.VMEM((n_blk // KEY_SPAN, keys, heads * rows), jnp.float32),
                pltpu.VMEM((hd, heads * rows), jnp.float32),
                pltpu.VMEM((hd, heads * rows), jnp.float32),
                pltpu.VMEM((keys, heads * rows), jnp.bfloat16),
                pltpu.VMEM((keys, heads * rows), jnp.bfloat16),
                pltpu.VMEM((keys, heads * rows), jnp.float32),
            ],
        ),
        out_shape=[head_shape, head_shape] + dkv_shapes,
        input_output_aliases=aliases,
        compiler_params=pltpu.CompilerParams(vmem_limit_bytes=56 * 1024 * 1024),
        cost_estimate=pl.CostEstimate(flops=24 * scores * hd, bytes_accessed=40_000_000, transcendentals=scores),
    )(*operands)


def solution(mesh):
    n_sp = mesh.shape['sp']

    def local_step(hid_loc, gout_loc, w_query, w_key, w_value, w_out):
        n_batch, seq_loc, d_model = hid_loc.shape
        n_heads, head_dim = w_query.shape[1:]
        full = n_heads * head_dim
        n_rows = n_batch * seq_loc
        me = lax.axis_index('sp')
        cos2, sin2 = rope_tables(me * seq_loc + jnp.arange(seq_loc), head_dim)
        w_kv = jnp.concatenate([w_key, w_value], axis=1)
        hid = hid_loc.reshape(n_rows, d_model)
        gout = gout_loc.reshape(n_rows, d_model)
        wo = w_out.reshape(full, d_model)
        kv = dot(hid, w_kv, NN).astype(jnp.bfloat16).reshape(n_batch, seq_loc, 2 * head_dim)
        k_f = kv[..., :head_dim].astype(jnp.float32)
        k_rot = (k_f * cos2 + swap_halves(k_f) * sin2).astype(jnp.bfloat16)
        kv = jnp.concatenate([k_rot, kv[..., head_dim:]], axis=-1)
        kv_all = lax.all_gather(kv, 'sp', axis=0, tiled=False)
        wq = w_query.reshape(d_model, full)
        q = dot(hid, wq, NN).astype(jnp.bfloat16).reshape(n_batch, seq_loc, full)
        do = dot(gout, wo, NT).astype(jnp.bfloat16).reshape(n_batch, seq_loc, full)
        me_arr = me.astype(jnp.int32).reshape(1)

        groups = HEAD_GROUPS
        n_groups = len(groups)
        dkv, os, dqs, dwo, dwq = None, [], [], [], []
        base = list(range(n_sp))
        start = 0
        for g, heads in enumerate(groups):
            last = g == n_groups - 1
            o_g, dq_g, *dkv = attend(start // heads, heads, me_arr, q, do, kv_all, cos2, sin2, dkv, last)
            dkv = dkv if last else dkv[0]
            start += heads
            o_g = o_g.reshape(n_rows, heads * head_dim)
            dq_g = dq_g.reshape(n_rows, heads * head_dim)
            os.append(o_g)
            dqs.append(dq_g)
            dwo.append(dot(o_g, gout, (((0,), (0,)), ((), ()))))
            dwq.append(dot(hid, dq_g, (((0,), (0,)), ((), ()))))
            if not last:
                order = [base[g + 1:] + base[:g + 1]]
                me_arr, dwo[g], dwq[g] = lax.optimization_barrier((me_arr, dwo[g], dwq[g]))
                if g > 0:
                    me_arr, dwo[g - 1], dwq[g - 1] = lax.optimization_barrier((me_arr, dwo[g - 1], dwq[g - 1]))
                dwo[g], dwq[g] = lax.psum((dwo[g], dwq[g]), 'sp', axis_index_groups=order)
        own, other = dkv
        chip = me // 2
        twin = lax.ppermute(other, 'sp', [(i, i ^ 1) for i in base])
        part = (own.astype(jnp.float32) + twin.astype(jnp.float32)).astype(jnp.bfloat16)
        part, os = lax.optimization_barrier((part, os))
        dkv_loc = lax.dynamic_index_in_dim(part, chip, 0, keepdims=False).astype(jnp.float32)
        for far in range(1, n_sp // 2):
            piece = lax.dynamic_index_in_dim(part, jnp.bitwise_xor(chip, far), 0, keepdims=False)
            piece = lax.ppermute(piece, 'sp', [(i, i ^ (2 * far)) for i in base])
            dkv_loc = dkv_loc + piece.astype(jnp.float32)
        attn_out = dot(jnp.concatenate(os, axis=1), wo, NN).astype(jnp.bfloat16)
        attn_out, dkv_loc = lax.optimization_barrier((attn_out, dkv_loc))
        dk_f = dkv_loc[..., :head_dim]
        dk_raw = (dk_f * cos2 - swap_halves(dk_f) * sin2).astype(jnp.bfloat16)
        dkv_raw = jnp.concatenate([dk_raw, dkv_loc[..., head_dim:].astype(jnp.bfloat16)], axis=-1).reshape(n_rows, 2 * head_dim)
        dw_kv = dot(hid, dkv_raw, (((0,), (0,)), ((), ())))
        dwq[-1] = dwq[-1].reshape(d_model, groups[-1], head_dim)
        dw_kv, dwo, dwq = lax.optimization_barrier((dw_kv, dwo, dwq))
        dwo[-1], dwq[-1], dw_kv = lax.psum((dwo[-1], dwq[-1], dw_kv), 'sp')
        d_hidden = (dot(jnp.concatenate(dqs, axis=1), wq, NT) + dot(dkv_raw, w_kv, NT)).astype(jnp.bfloat16)
        dw_query = jnp.zeros(w_query.shape, jnp.float32)
        dw_out = jnp.zeros((full, d_model), jnp.float32)
        start = 0
        for heads, w_q, w_o in zip(groups, dwq, dwo):
            dw_query = lax.dynamic_update_slice(dw_query, w_q.reshape(d_model, heads, head_dim), (0, start, 0))
            dw_out = lax.dynamic_update_slice(dw_out, w_o, (start * head_dim, 0))
            start += heads
        return (attn_out.reshape(hid_loc.shape), d_hidden.reshape(hid_loc.shape), dw_query, dw_kv[:, :head_dim], dw_kv[:, head_dim:], dw_out.reshape(n_heads, head_dim, d_model))

    act_spec = P('dp', 'sp', None)
    return jax.shard_map(local_step, mesh=mesh, in_specs=(act_spec, act_spec, P(), P(), P(), P()), out_specs=(act_spec, act_spec, P('dp', None, None), P('dp', None), P('dp', None), P('dp', None, None)), check_vma=False)
```

time: 874 us -> 878 us (level)
  waiting for transfers between devices: 468 us -> 342 us
  local copies, waits for them, and re-layouts: 50.8 us -> 124 us
  starting transfers between devices: 0.41 us -> 55.7 us
  Pallas kernels: 113 us -> 150 us
  matrix products: 197 us -> 176 us
  other arithmetic: 25.7 us -> 9.09 us
    dynamic_update_slice x0 -> x6, local copies, waits for them, and re-layouts: none -> 89.7 us  [the longest x3 72.9 us: local_step(): lax.dynamic_update_slice(dw_query, w_q.reshape(d_model, heads, head_dim),...]
    psum x1, waiting for transfers between devices: 107 us -> 21.6 us  [local_step(): dwo[-1], dwq[-1], dw_kv = lax.psum((dwo[-1], dwq[-1], dw_kv), 'sp')]
    ppermute x0 -> x4, starting transfers between devices: none -> 55.3 us  [the longest x3 55.3 us: local_step(): piece = lax.ppermute(piece, 'sp', [(i, i ^ 2 * far) for i in base])]
    ppermute x0 -> x4, waiting for transfers between devices: none -> 54 us  [the longest x3 54 us: local_step(): piece = lax.ppermute(piece, 'sp', [(i, i ^ 2 * far) for i in base])]
    reduce_scatter x1 -> x0, waiting for transfers between devices: 49.2 us -> none  [local_step(): dkv_loc = lax.psum_scatter(dkv, 'sp', scatter_dimension=0, tiled=False)]
    psum x3 -> x2, waiting for transfers between devices: 306 us -> 261 us  [local_step(): dwo[g], dwq[g] = lax.psum((dwo[g], dwq[g]), 'sp', axis_index_groups=order)]
    pallas_call x4 -> x3, Pallas kernels: 113 us -> 150 us  [attend(): pl.pallas_call(functools.partial(attn_kernel, heads, first, last), grid_s...]
    concatenate x2 -> x0, other arithmetic: 21.6 us -> none  [the longest x1 14.5 us: local_step(): jnp.concatenate([w.reshape(d_model, heads, head_dim) for w in dwq], axis=1)]
  transfers between devices with their start and end apart: 6 -> 8, of which waited for: 6 -> 7; matrix products, arithmetic and copies ran while one was open for 21% -> 28% of each run, Pallas kernels for 10% -> 6%
where the time goes in v2:
time: 878 us; the launch traced here: 872 us
  waiting for transfers between devices  342 us (39%)
  matrix products  176 us (20%)
  Pallas kernels  150 us (17%)
  local copies, waits for them, and re-layouts  124 us (14%)
  starting transfers between devices  55.7 us (6%)
  between operations  14.6 us (2%)
  other arithmetic  9.09 us (1%)
    psum x2, waiting for transfers between devices, local_step(): dwo[g], dwq[g] = lax.psum((dwo[g], dwq[g]), 'sp', axis_index_groups=order)  261 us
    dot_general x13, matrix products, dot(): return lax.dot_general(a, b, dims, preferred_element_type=jnp.float32)  176 us
    pallas_call x3, Pallas kernels, attend(): pl.pallas_call(functools.partial(attn_kernel, heads, first, last), grid_s...  150 us
    dynamic_update_slice x3, local copies, waits for them, and re-layouts, local_step(): lax.dynamic_update_slice(dw_query, w_q.reshape(d_model, heads, head_dim),...  72.9 us
    ppermute x3, starting transfers between devices, local_step(): piece = lax.ppermute(piece, 'sp', [(i, i ^ 2 * far) for i in base])  55.3 us
    ppermute x3, waiting for transfers between devices, local_step(): piece = lax.ppermute(piece, 'sp', [(i, i ^ 2 * far) for i in base])  54 us
    psum x1, waiting for transfers between devices, local_step(): dwo[-1], dwq[-1], dw_kv = lax.psum((dwo[-1], dwq[-1], dw_kv), 'sp')  21.6 us
  transfers between devices with their start and end apart: 8, of which 7 were waited for; matrix products, arithmetic and copies ran while one was open for 28% of the time, Pallas kernels for 6%

profile of v2, /device:TPU:0, one launch (start us, length us, event | category | flops | bytes accessed | tf_op | source)
XLA Modules:
  0.0 871.6 jit_solution(6964001595637552869)
XLA Ops:
  7.2 1.1 constant_dynamic-update-slice_fusion.1
  8.4 1.2 constant_dynamic-update-slice_fusion
  9.6 1.0 copy-done.3
  10.5 5.8 fusion.22
  16.3 0.5 copy.26
  16.8 1.0 slice_convert_fusion.1
  18.1 0.5 multiply_cosine_fusion
  19.3 2.2 pad_maximum_fusion
  21.7 23.7 %convolution_convert_fusion = bf16[2048,2048]{1,0:T(8,128)(2,1)} fusion(bf16[2048,2048]{1,0:T(8,128)(2,1)} %bitcast.96, bf16[2048,2048]{1,0:T(8,128)(2,1)} %bitcast.97), kind=kOutput, calls=%fused_computation.18 | convolution fusion | flops 17184063488 | bytes 25165824 | tf_op jit(solution)/shard_map/dot_general | solution.py:19
  45.4 23.4 %fusion.17 = bf16[2048,2048]{1,0:T(8,128)(2,1)} fusion(bf16[2048,2048]{1,0:T(8,128)(2,1)} %bitcast.85, bf16[256,8,16,128]{3,2,1,0:T(8,128)(2,1)} %bitcast.101), kind=kOutput, calls=%fused_computation.17 | convolution fusion | flops 17184063488 | bytes 25165824 | tf_op jit(solution)/shard_map/dot_general | solution.py:19
  68.8 5.8 all-gather.3.cloned.1.call-done
  74.6 54.2 %shard_map.109 = (bf16[8,256,768]{2,1,0:T(8,128)(2,1)}, bf16[8,256,768]{2,1,0:T(8,128)(2,1)}, f32[8,8,256,256]{3,2,1,0:T(8,128)}) custom-call(s32[1]{0:T(128)} %bitcast.blk_ref, bf16[8,256,2048]{2,1,0:T(8,128)(2,1)} %bitcast.110, bf16[8,256,2048]{2,1,0:T(8,128)(2,1)} %bitcast.107, bf16[8,8,256,256]{3,2,1,0:T(8,128)(2,1)} %bitcast.103, f32[256,128]{1,0:T(8,128)} %copy-done.5, ...), custom_call_target="tpu_custom_call" | custom-call | flops 77309411328 | bytes 40000000 | tf_op jit(solution)/shard_map/pallas_call | solution.py:192
  128.8 11.9 %convolution_bitcast_fusion.3 = f32[768,2048]{1,0:T(8,128)} fusion(bf16[8,256,768]{2,1,0:T(8,128)(2,1)} %get-tuple-element.38, bf16[8,256,2048]{2,1,0:T(8,128)(2,1)} %param.7), kind=kOutput, calls=%fused_computation.24 | convolution fusion | flops 6442450944 | bytes 17825792 | tf_op jit(solution)/shard_map/dot_general | solution.py:19
  140.7 8.9 %convolution_bitcast_fusion.2 = f32[2048,768]{0,1:T(8,128)} fusion(bf16[8,256,768]{2,1,0:T(8,128)(2,1)S(1)} %copy-done.9, bf16[8,256,2048]{2,1,0:T(8,128)(2,1)S(1)} %copy-done), kind=kOutput, calls=%fused_computation.23 | convolution fusion | flops 6442450944 | bytes 17825792 | tf_op jit(solution)/shard_map/dot_general | solution.py:19
  149.7 55.4 %shard_map.110 = (bf16[8,256,768]{2,1,0:T(8,128)(2,1)}, bf16[8,256,768]{2,1,0:T(8,128)(2,1)}, f32[8,8,256,256]{3,2,1,0:T(8,128)}) custom-call(s32[1]{0:T(128)} %bitcast.blk_ref, bf16[8,256,2048]{2,1,0:T(8,128)(2,1)} %bitcast.111, bf16[8,256,2048]{2,1,0:T(8,128)(2,1)} %bitcast.108, ...), custom_call_target="tpu_custom_call", output_to_operand_aliasing={{2}: (6, {})} | custom-call | flops 77309411328 | bytes 40000000 | tf_op jit(solution)/shard_map/pallas_call | solution.py:192
  205.1 12.0 %convolution_bitcast_fusion.1 = f32[768,2048]{1,0:T(8,128)} fusion(bf16[8,256,768]{2,1,0:T(8,128)(2,1)} %get-tuple-element.42, bf16[8,256,2048]{2,1,0:T(8,128)(2,1)} %param.7), kind=kOutput, calls=%fused_computation.22 | convolution fusion | flops 6442450944 | bytes 17825792 | tf_op jit(solution)/shard_map/dot_general | solution.py:19
  217.1 11.2 %convolution_bitcast_fusion = f32[2048,768]{0,1:T(8,128)} fusion(bf16[8,256,768]{2,1,0:T(8,128)(2,1)S(1)} %copy-done.10, bf16[8,256,2048]{2,1,0:T(8,128)(2,1)} %param.6), kind=kOutput, calls=%fused_computation.21 | convolution fusion | flops 6442450944 | bytes 17825792 | tf_op jit(solution)/shard_map/dot_general | solution.py:19
  228.3 157.2 %all-reduce.11.cloned.1.call-done = (f32[768,2048]{1,0:T(8,128)}, f32[2048,768]{0,1:T(8,128)}) async-done(((f32[768,2048]{1,0:T(8,128)}, f32[2048,768]{0,1:T(8,128)}), (f32[768,2048]{1,0:T(8,128)}, f32[2048,768]{0,1:T(8,128)})) %all-reduce.11.cloned.1.call-update) | async-done | bytes 12582928 | tf_op jit(solution)/shard_map/psum | solution.py:262
  385.4 40.4 %shard_map.111 = (bf16[8,256,512]{2,1,0:T(8,128)(2,1)}, bf16[8,256,512]{2,1,0:T(8,128)(2,1)}, bf16[4,8,256,256]{3,2,1,0:T(8,128)(2,1)}, bf16[4,8,256,256]{3,2,1,0:T(8,128)(2,1)}) custom-call(s32[1]{0:T(128)} %bitcast.blk_ref, bf16[8,256,2048]{2,1,0:T(8,128)(2,1)} %bitcast.112, bf16[8,256,2048]{2,1,0:T(8,128)(2,1)} %bitcast.109, ...), custom_call_target="tpu_custom_call" | custom-call | flops 51539607552 | bytes 40000000 | tf_op jit(solution)/shard_map/pallas_call | solution.py:192
  426.1 1.4 copy-done.12
  427.5 9.8 %convolution_bitcast_fusion.4 = f32[512,2048]{1,0:T(8,128)} fusion(bf16[8,256,512]{2,1,0:T(8,128)(2,1)S(1)} %copy-done.12, bf16[8,256,2048]{2,1,0:T(8,128)(2,1)} %param.7), kind=kOutput, calls=%fused_computation.25 | convolution fusion | flops 4294967296 | bytes 14680064 | tf_op jit(solution)/shard_map/dot_general | solution.py:19
  437.3 9.6 %fusion.36 = f32[512,2048,1]{1,0,2:T(8,128)} fusion(bf16[8,256,512]{2,1,0:T(8,128)(2,1)S(1)} %copy-done.11, bf16[8,256,2048]{2,1,0:T(8,128)(2,1)} %param.6), kind=kOutput, calls=%fused_computation.63 | convolution fusion | flops 4294967296 | bytes 14680064 | tf_op jit(solution)/shard_map/dot_general | solution.py:19
  446.9 3.9 add_convert_fusion.1
  451.1 54.7 %collective-permute-start.3 = (bf16[8,256,256]{2,1,0:T(8,128)(2,1)S(1)}, bf16[8,256,256]{2,1,0:T(8,128)(2,1)S(1)}, u32[]{:S(2)}, u32[]{:S(2)}) collective-permute-start(bf16[8,256,256]{2,1,0:T(8,128)(2,1)S(1)} %get-tuple-element.90), channel_id=1, source_target_pairs={{0,6},{1,7},{2,4},{3,5},{4,2},{5,3},{6,0},{7,1},{8,14},{9,15},{10,... | collective-permute-start | bytes 3145736 | tf_op jit(solution)/shard_map/ppermute | solution.py:271
  505.8 0.6 collective-permute-start.1
  506.4 21.6 %fusion.14 = bf16[2048,2048]{1,0:T(8,128)(2,1)} fusion(bf16[2048,2048]{1,0:T(8,128)(2,1)S(1)} %bitcast.100, bf16[2048,512]{1,0:T(8,128)(2,1)} %bitcast.119, bf16[2048,768]{1,0:T(8,128)(2,1)} %bitcast.117, bf16[2048,768]{1,0:T(8,128)(2,1)} %bitcast.116), kind=kOutput, calls=%fused_computation.16 | convolution fusion | flops 17209229312 | bytes 25165824 | tf_op jit(solution)/shard_map/dot_general | solution.py:19
  528.0 11.5 %collective-permute-done.3 = bf16[8,256,256]{2,1,0:T(8,128)(2,1)S(1)} collective-permute-done((bf16[8,256,256]{2,1,0:T(8,128)(2,1)S(1)}, bf16[8,256,256]{2,1,0:T(8,128)(2,1)S(1)}, u32[]{:S(2)}, u32[]{:S(2)}) %collective-permute-start.3) | collective-permute-done | bytes 1048608 | tf_op jit(solution)/shard_map/ppermute | solution.py:271
  539.5 34.8 %collective-permute-done.2 = bf16[8,256,256]{2,1,0:T(8,128)(2,1)S(1)} collective-permute-done((bf16[8,256,256]{2,1,0:T(8,128)(2,1)S(1)}, bf16[8,256,256]{2,1,0:T(8,128)(2,1)S(1)}, u32[]{:S(2)}, u32[]{:S(2)}) %collective-permute-start.2) | collective-permute-done | bytes 1048608 | tf_op jit(solution)/shard_map/ppermute | solution.py:271
  574.3 7.7 collective-permute-done.1
  582.0 0.5 fusion.24
  583.4 1.4 slice-done.1
  584.8 3.7 convolution_bitcast_fusion.5
  588.5 103.6 %all-reduce.13.cloned.1.call-done = (f32[768,2048]{1,0:T(8,128)}, f32[2048,768]{0,1:T(8,128)}) async-done(((f32[768,2048]{1,0:T(8,128)}, f32[2048,768]{0,1:T(8,128)}), (f32[768,2048]{1,0:T(8,128)}, f32[2048,768]{0,1:T(8,128)})) %all-reduce.13.cloned.1.call-update) | async-done | bytes 12582928 | tf_op jit(solution)/shard_map/psum | solution.py:262
  692.1 5.4 copy.36
  697.6 11.4 %dynamic_update_slice.21 = f32[2048,2048]{1,0:T(8,128)} pad(f32[768,2048]{1,0:T(8,128)} %get-tuple-element.67, f32[]{:T(128)} %constant.46.clone.1), padding=0_1280x0_0 | pad | bytes 23068676 | tf_op jit(solution)/shard_map/dynamic_update_slice | solution.py:288
  708.9 3.1 constant_dynamic-update-slice_fusion.3
  712.2 8.4 copy.34
  720.6 9.6 %dynamic_update_slice.18 = f32[2048,16,128]{2,1,0:T(8,128)} pad(f32[2048,6,128]{2,1,0:T(8,128)} %copy.34, f32[]{:T(128)} %constant.46.clone.1), padding=0_0x0_10x0_0 | pad | bytes 23068676 | tf_op jit(solution)/shard_map/dynamic_update_slice | solution.py:287
  730.1 8.4 copy.35
  738.5 59.3 %dynamic_update_slice.19 = f32[2048,16,128]{2,1,0:T(8,128)} dynamic-update-slice(f32[2048,16,128]{2,1,0:T(8,128)} %dynamic_update_slice.18, f32[2048,6,128]{2,1,0:T(8,128)} %copy.35, s32[]{:T(128)} %constant.41.clone.1, s32[]{:T(128)} %constant.47.clone.1, s32[]{:T(128)} %constant.41.clone.1) | dynamic-update-slice | bytes 12582916 | tf_op jit(solution)/shard_map/dynamic_update_slice | solution.py:287
  797.8 8.1 fusion.35
  805.9 26.0 %add_convert_fusion = bf16[2048,2048]{1,0:T(8,128)(2,1)} fusion(f32[2048,2048]{1,0:T(8,128)} %fusion.35, bf16[2048,512]{1,0:T(8,128)(2,1)} %bitcast.118, bf16[2048,768]{1,0:T(8,128)(2,1)} %bitcast.115, bf16[2048,768]{1,0:T(8,128)(2,1)} %bitcast.114, bf16[256,8,16,128]{3,2,1,0:T(8,128)(2,1)} %bitcast.102), kind=kOutput, calls=%fused_computation | convolution fusion | flops 17213423616 | bytes 41943040 | tf_op jit(solution)/shard_map/dot_general | solution.py:19
  831.9 21.6 %all-reduce.9.cloned.1.call-done = (f32[2048,4,128]{2,1,0:T(4,128)}, f32[2048,256]{0,1:T(8,128)}, f32[512,2048]{1,0:T(8,128)}) async-done(((f32[2048,4,128]{2,1,0:T(4,128)}, f32[2048,256]{0,1:T(8,128)}, f32[512,2048]{1,0:T(8,128)}), (f32[2048,4,128]{2,1,0:T(4,128)}, f32[2048,256]{0,1:T(8,128)}, f32[512,2048]{1,0:T(8,128)})) %all-reduce.9.cloned.1.call-update) | async-done | bytes 10485776 | tf_op jit(solution)/shard_map/psum | solution.py:281
  853.5 1.7 fusion.32
  855.2 1.3 copy.37
  856.5 1.3 copy.38
  857.8 4.1 constant_dynamic-update-slice_fusion.4
  862.3 2.3 constant_dynamic-update-slice_fusion.2
  (59 shorter events, 3.0 us)
Async XLA Ops:
  7.2 67.4 %all-gather.3.cloned.1.call-start = ((), (), s32[]{:S(2)}) async-start(), calls=%async_computation | async-start | bytes 9437184 | tf_op jit(solution)/shard_map/all_gather | solution.py:235
  9.5 1.0 copy-start.3
  18.8 26.5 %copy-start.5 = (f32[256,128]{1,0:T(8,128)}, f32[256,128]{1,0:T(8,128)S(1)}, u32[]{:S(2)}) copy-start(f32[256,128]{1,0:T(8,128)S(1)} %get-tuple-element.103.cos_ref) | copy-start | bytes 393220
  18.8 26.5 %copy-start.7 = (f32[256,128]{1,0:T(8,128)}, f32[256,128]{1,0:T(8,128)S(1)}, u32[]{:S(2)}) copy-start(f32[256,128]{1,0:T(8,128)S(1)} %get-tuple-element.104.sin_ref) | copy-start | bytes 393220
  21.4 364.0 %all-reduce.11.cloned.1.call-start = ((), (), s32[]{:S(2)}) async-start(), calls=%async_computation.2 | async-start | bytes 25165824 | tf_op jit(solution)/shard_map/psum | solution.py:262
  128.8 11.9 %copy-start = (bf16[8,256,2048]{2,1,0:T(8,128)(2,1)S(1)}, bf16[8,256,2048]{2,1,0:T(8,128)(2,1)}, u32[]{:S(2)}) copy-start(bf16[8,256,2048]{2,1,0:T(8,128)(2,1)} %param.6) | copy-start | bytes 25165828
  128.8 11.9 %copy-start.9 = (bf16[8,256,768]{2,1,0:T(8,128)(2,1)S(1)}, bf16[8,256,768]{2,1,0:T(8,128)(2,1)}, u32[]{:S(2)}) copy-start(bf16[8,256,768]{2,1,0:T(8,128)(2,1)} %get-tuple-element.39) | copy-start | bytes 9437188
  149.7 542.4 %all-reduce.13.cloned.1.call-start = ((), (), s32[]{:S(2)}) async-start(), calls=%async_computation.3 | async-start | bytes 25165824 | tf_op jit(solution)/shard_map/psum | solution.py:262
  205.1 12.0 %copy-start.10 = (bf16[8,256,768]{2,1,0:T(8,128)(2,1)S(1)}, bf16[8,256,768]{2,1,0:T(8,128)(2,1)}, u32[]{:S(2)}) copy-start(bf16[8,256,768]{2,1,0:T(8,128)(2,1)} %get-tuple-element.43) | copy-start | bytes 9437188
  425.9 1.6 copy-start.12
  425.9 21.0 %collective-permute-start = (bf16[4,8,256,256]{3,2,1,0:T(8,128)(2,1)}, bf16[4,8,256,256]{3,2,1,0:T(8,128)(2,1)}, u32[]{:S(2)}, u32[]{:S(2)}) collective-permute-start(bf16[4,8,256,256]{3,2,1,0:T(8,128)(2,1)} %get-tuple-element.50), channel_id=1, source_target_pairs={{0,1},{1,0},{2,3},{3,2},{4,5},{5,4},{6,7},{7,6},{8,9},{9,8},{10,11... | collective-permute-start | bytes 12582920 | tf_op jit(solution)/shard_map/ppermute | solution.py:265
  426.0 427.5 %all-reduce.9.cloned.1.call-start = ((), (), s32[]{:S(2)}) async-start(), calls=%async_computation.1 | async-start | bytes 20971520 | tf_op jit(solution)/shard_map/psum | solution.py:281
  427.5 9.8 %copy-start.11 = (bf16[8,256,512]{2,1,0:T(8,128)(2,1)S(1)}, bf16[8,256,512]{2,1,0:T(8,128)(2,1)}, u32[]{:S(2)}) copy-start(bf16[8,256,512]{2,1,0:T(8,128)(2,1)} %get-tuple-element.57) | copy-start | bytes 6291460
  437.3 9.6 %copy-start.1 = (bf16[4,8,256,256]{3,2,1,0:T(8,128)(2,1)S(1)}, bf16[4,8,256,256]{3,2,1,0:T(8,128)(2,1)}, u32[]{:S(2)}) copy-start(bf16[4,8,256,256]{3,2,1,0:T(8,128)(2,1)} %get-tuple-element.49) | copy-start | bytes 12582916
  437.3 69.1 %slice-start.4 = ((s8[8388608]{0:T(1024)(128)(4,1)}), s8[4194304]{0:T(1024)(128)(4,1)S(1)}, s32[]{:S(2)}) async-start(s8[8388608]{0:T(1024)(128)(4,1)} %bitcast.98), calls=%async_computation.8 | async-start | bytes 8388608
  446.9 59.5 %slice-start.5 = ((s8[8388608]{0:T(1024)(128)(4,1)}), s8[4194304]{0:T(1024)(128)(4,1)S(1)}, s32[]{:S(2)}) async-start(s8[8388608]{0:T(1024)(128)(4,1)} %bitcast.98), calls=%async_computation.9 | async-start | bytes 8388608
  451.1 88.4 %collective-permute-start.3 = (bf16[8,256,256]{2,1,0:T(8,128)(2,1)S(1)}, bf16[8,256,256]{2,1,0:T(8,128)(2,1)S(1)}, u32[]{:S(2)}, u32[]{:S(2)}) collective-permute-start(bf16[8,256,256]{2,1,0:T(8,128)(2,1)S(1)} %get-tuple-element.90), channel_id=1, source_target_pairs={{0,6},{1,7},{2,4},{3,5},{4,2},{5,3},{6,0},{7,1},{8,14},{9,15},{10,... | collective-permute-start | bytes 3145736 | tf_op jit(solution)/shard_map/ppermute | solution.py:271
  505.8 68.6 %collective-permute-start.2 = (bf16[8,256,256]{2,1,0:T(8,128)(2,1)S(1)}, bf16[8,256,256]{2,1,0:T(8,128)(2,1)S(1)}, u32[]{:S(2)}, u32[]{:S(2)}) collective-permute-start(bf16[8,256,256]{2,1,0:T(8,128)(2,1)S(1)} %get-tuple-element.91), channel_id=1, source_target_pairs={{0,4},{1,5},{2,6},{3,7},{4,0},{5,1},{6,2},{7,3},{8,12},{9,13},{10,... | collective-permute-start | bytes 3145736 | tf_op jit(solution)/shard_map/ppermute | solution.py:271
  505.8 76.2 %collective-permute-start.1 = (bf16[8,256,256]{2,1,0:T(8,128)(2,1)S(1)}, bf16[8,256,256]{2,1,0:T(8,128)(2,1)S(1)}, u32[]{:S(2)}, u32[]{:S(2)}) collective-permute-start(bf16[8,256,256]{2,1,0:T(8,128)(2,1)S(1)} %get-tuple-element.89), channel_id=1, source_target_pairs={{0,2},{1,3},{2,0},{3,1},{4,6},{5,7},{6,4},{7,5},{8,10},{9,11},{10,... | collective-permute-start | bytes 3145736 | tf_op jit(solution)/shard_map/ppermute | solution.py:271
  527.9 55.0 %copy-start.6 = (f32[256,128]{1,0:T(8,128)S(1)}, f32[256,128]{1,0:T(8,128)}, u32[]{:S(2)}) copy-start(f32[256,128]{1,0:T(8,128)} %copy-done.5) | copy-start | bytes 393220
  528.0 55.0 %copy-start.8 = (f32[256,128]{1,0:T(8,128)S(1)}, f32[256,128]{1,0:T(8,128)}, u32[]{:S(2)}) copy-start(f32[256,128]{1,0:T(8,128)} %copy-done.7) | copy-start | bytes 393220
  528.0 55.4 %slice-start = ((s8[8388608]{0:T(1024)(128)(4,1)}), s8[4194304]{0:T(1024)(128)(4,1)S(1)}, s32[]{:S(2)}) async-start(s8[8388608]{0:T(1024)(128)(4,1)} %bitcast.86), calls=%async_computation.4 | async-start | bytes 8388608
  582.6 2.2 slice-start.1
  692.1 16.8 %slice-start.2 = ((s8[6291456]{0:T(1024)(128)(4,1)}), s8[2097152]{0:T(1024)(128)(4,1)S(1)}, s32[]{:S(2)}) async-start(s8[6291456]{0:T(1024)(128)(4,1)} %bitcast.92), calls=%async_computation.6 | async-start | bytes 4194304
  697.5 11.4 %slice-start.3 = ((s8[6291456]{0:T(1024)(128)(4,1)}), s8[4194304]{0:T(1024)(128)(4,1)S(1)}, s32[]{:S(2)}) async-start(s8[6291456]{0:T(1024)(128)(4,1)} %bitcast.92), calls=%async_computation.7 | async-start | bytes 8388608
  738.5 59.3 %copy-start.4 = (bf16[2048,256]{1,0:T(8,128)(2,1)S(1)}, bf16[2048,256]{1,0:T(8,128)(2,1)}, u32[]{:S(2)}) copy-start(bf16[2048,256]{1,0:T(8,128)(2,1)} %copy-done.3) | copy-start | bytes 3145732
  857.8 4.4 copy-start.2
Sparse Core Ops, SparseCore 0:
  21.6 52.9 all-gather.2
  149.8 235.6 all-reduce.10
  426.1 265.9 all-reduce.12
  712.2 141.3 all-reduce.8
